TPU v7x, 32 devices: a whole 2x2x4 slice. The times are simulated.
32 devices in a mesh: rep: 2 (over x), fsdp: 16 (over z, y, core).
Axes of the slice: x: 2, y: 2, z: 4, core: 2. Of those that a mesh axis runs over, the one named last changes fastest.
Arguments:
- layer_input: bfloat16 [4096, 2048], P(('rep', 'fsdp')), may hold values from -6 to 6
- segment: int32 [32, 128], P(('rep', 'fsdp')), may hold values from 0 to 1, as said below
- live_mask: int32 [32, 128], P(('rep', 'fsdp')), may hold values from 0 to 1, as said below
- attention_gain: bfloat16 [2048], P('fsdp'), may hold values from 0.099609375 to 1.8984375
- attention_shift: bfloat16 [2048], P('fsdp'), may hold values from -4 to 4
- joined_weight: bfloat16 [2048, 6144], P('fsdp'), may hold values from -0.125 to 0.125
- joined_bias: bfloat16 [6144], P('fsdp'), may hold values from -4 to 4
- output_weight: bfloat16 [2048, 2048], P('fsdp'), may hold values from -0.375 to 0.375
- output_bias: bfloat16 [2048], P('fsdp'), may hold values from -4 to 4
- feedforward_gain: bfloat16 [2048], P('fsdp'), may hold values from 0.099609375 to 1.8984375
- feedforward_shift: bfloat16 [2048], P('fsdp'), may hold values from -4 to 4
- expand_weight: bfloat16 [2048, 8192], P('fsdp'), may hold values from -0.125 to 0.125
- expand_bias: bfloat16 [8192], P('fsdp'), may hold values from -4 to 4
- shrink_weight: bfloat16 [8192, 2048], P('fsdp'), may hold values from -0.0625 to 0.0625
- shrink_bias: bfloat16 [2048], P('fsdp'), may hold values from -4 to 4
- cotangent: bfloat16 [4096, 2048], P(('rep', 'fsdp')), may hold values from -6 to 6
Outputs:
- layer_output: bfloat16 [4096, 2048], P(('rep', 'fsdp'))
- input_grad: bfloat16 [4096, 2048], P(('rep', 'fsdp'))
- attention_gain_grad: float32 [2048], P('fsdp')
- attention_shift_grad: float32 [2048], P('fsdp')
- joined_weight_grad: float32 [2048, 6144], P('fsdp')
- joined_bias_grad: float32 [6144], P('fsdp')
- output_weight_grad: float32 [2048, 2048], P('fsdp')
- output_bias_grad: float32 [2048], P('fsdp')
- feedforward_gain_grad: float32 [2048], P('fsdp')
- feedforward_shift_grad: float32 [2048], P('fsdp')
- expand_weight_grad: float32 [2048, 8192], P('fsdp')
- expand_bias_grad: float32 [8192], P('fsdp')
- shrink_weight_grad: float32 [8192, 2048], P('fsdp')
- shrink_bias_grad: float32 [2048], P('fsdp')
Inputs may be any that keep to these rules, and one draw needn't show every extreme that they name: `segment`: within each slot the number is 0 on a first sequence of 32 to 128 positions and 1 after it, never falling; in at least one slot the first sequence fills all 128 positions, not always the same slot. `live_mask`: in each slot the 1s form a prefix that covers the first sequence; positions after it are padding. At least one slot is live in all 128 positions.
All inputs are finite; a program needn't handle non-finite values.
Results may differ from a plain program's by a relative error of at most 0.0095.
Values may be sent and summed in bfloat16 or wider, within the bound.
A program may use at most 448 MiB of HBM per device.

v0:
```python
import jax
import jax.numpy as jnp
from jax import lax
from jax.sharding import PartitionSpec as P

D = 2048
HEADS = 16
HEAD_DIM = 128
ROT = 32


epsilon = 1e-05
masked_score = -1e30
rotary_base = 10000.0


def as_sent(shard):
    return jax.tree.map(lambda a: a.astype(jnp.bfloat16) if a.dtype == jnp.float32 else a, shard)


def norm_rows(rows, gain, shift):
    centre = jnp.mean(rows, -1, keepdims=True)
    centred = rows - centre
    inverse = lax.rsqrt(jnp.mean(centred * centred, -1, keepdims=True) + epsilon)
    normalized = centred * inverse
    return (normalized * gain.astype(jnp.float32) + shift.astype(jnp.float32), normalized, inverse)


def norm_back(normed_grad, normalized, inverse, gain):
    scaled = normed_grad * gain.astype(jnp.float32)
    row_grad = inverse * (
        scaled
        - jnp.mean(scaled, -1, keepdims=True)
        - normalized * jnp.mean(scaled * normalized, -1, keepdims=True)
    )
    return (row_grad, jnp.sum(normed_grad * normalized, 0), jnp.sum(normed_grad, 0))


def rotary_tables(segment):
    length = segment.shape[-1]
    places = jnp.arange(length, dtype=jnp.int32)
    earlier = jnp.sum((segment[..., None, :] < segment[..., :, None]).astype(jnp.int32), -1)
    position = (places - earlier).astype(jnp.float32)
    exponent = jnp.arange(ROT // 2, dtype=jnp.float32) * 2.0 / ROT
    frequency = jnp.power(jnp.float32(rotary_base), -exponent)
    angle = position[..., None] * frequency
    return (jnp.cos(angle), jnp.sin(angle))


def turn(heads, cosine, sine, sign):
    half = ROT // 2
    front = heads[..., :half]
    behind = heads[..., half:ROT]
    cos_wide = cosine[..., None, :]
    sin_wide = sine[..., None, :] * sign
    return jnp.concatenate(
        [
            front * cos_wide - behind * sin_wide,
            behind * cos_wide + front * sin_wide,
            heads[..., ROT:],
        ],
        -1,
    )


def gelu_slope(values):
    return (
        0.5 * (1.0 + lax.erf(values * 0.7071067811865476))
        + values * jnp.exp(-0.5 * values * values) * 0.3989422804014327
    )


def attention_inputs(rows, weights, cosine, sine):
    gain, shift, joined_weight, joined_bias = (weights[0], weights[1], weights[2], weights[3])
    normed, normalized, inverse = norm_rows(rows, gain, shift)
    normed_low = normed.astype(jnp.bfloat16)
    joined = jnp.dot(
        normed_low, joined_weight, preferred_element_type=jnp.float32
    ) + joined_bias.astype(jnp.float32)
    length = rows.shape[0]
    split = joined.reshape(length, 3, HEADS, HEAD_DIM)
    queries = turn(split[:, 0], cosine, sine, 1.0).astype(jnp.bfloat16)
    keys = turn(split[:, 1], cosine, sine, 1.0).astype(jnp.bfloat16)
    values = split[:, 2].astype(jnp.bfloat16)
    return (normed_low, normalized, inverse, queries, keys, values)


def score_block(queries, keys, allowed):
    scores = jnp.einsum(
        "thd,shd->hts", queries, keys, preferred_element_type=jnp.float32
    ) * HEAD_DIM ** (-0.5)
    return jnp.where(allowed[None], scores, masked_score)


def feedforward_inputs(rows, weights):
    gain, shift, expand_weight, expand_bias = (weights[0], weights[1], weights[2], weights[3])
    normed, normalized, inverse = norm_rows(rows, gain, shift)
    normed_low = normed.astype(jnp.bfloat16)
    expanded = jnp.dot(
        normed_low, expand_weight, preferred_element_type=jnp.float32
    ) + expand_bias.astype(jnp.float32)
    return (normed_low, normalized, inverse, expanded)


def body(
    layer_input,
    segment,
    live_mask,
    attention_gain,
    attention_shift,
    joined_weight,
    joined_bias,
    output_weight,
    output_bias,
    feedforward_gain,
    feedforward_shift,
    expand_weight,
    expand_bias,
    shrink_weight,
    shrink_bias,
    cotangent,
):
    rows = layer_input.astype(jnp.float32)
    seg_row = segment[0]
    live_rows = live_mask[0].astype(jnp.float32)[:, None]
    length = seg_row.shape[0]
    cosine, sine = rotary_tables(seg_row)
    places = jnp.arange(length, dtype=jnp.int32)
    allowed = (seg_row[:, None] == seg_row[None, :]) & (places[None, :] <= places[:, None])
    attention_parts = (
        attention_gain,
        attention_shift,
        joined_weight,
        joined_bias,
        output_weight,
        output_bias,
    )
    feedforward_parts = (
        feedforward_gain,
        feedforward_shift,
        expand_weight,
        expand_bias,
        shrink_weight,
        shrink_bias,
    )
    attention_full = (
        lax.all_gather(attention_gain, "fsdp", axis=0, tiled=True),
        lax.all_gather(attention_shift, "fsdp", axis=0, tiled=True),
        lax.all_gather(joined_weight, "fsdp", axis=0, tiled=True),
        lax.all_gather(joined_bias, "fsdp", axis=0, tiled=True),
        lax.all_gather(output_weight, "fsdp", axis=0, tiled=True),
        lax.all_gather(output_bias, "fsdp", axis=0, tiled=True),
    )
    feedforward_full = (
        lax.all_gather(feedforward_gain, "fsdp", axis=0, tiled=True),
        lax.all_gather(feedforward_shift, "fsdp", axis=0, tiled=True),
        lax.all_gather(expand_weight, "fsdp", axis=0, tiled=True),
        lax.all_gather(expand_bias, "fsdp", axis=0, tiled=True),
        lax.all_gather(shrink_weight, "fsdp", axis=0, tiled=True),
        lax.all_gather(shrink_bias, "fsdp", axis=0, tiled=True),
    )
    normed_one, normalized_one, inverse_one, queries, keys, values = attention_inputs(
        rows, attention_full, cosine, sine
    )
    scores = score_block(queries, keys, allowed)
    top = jnp.max(scores, -1, keepdims=True)
    expo = jnp.exp(scores - top)
    total = jnp.sum(expo, -1, keepdims=True)
    log_total = top + jnp.log(total)
    probs_low = (expo / total).astype(jnp.bfloat16)
    mixed = jnp.einsum("hts,shd->thd", probs_low, values, preferred_element_type=jnp.float32)
    mixed = mixed.reshape(length, D).astype(jnp.bfloat16)
    attended = jnp.dot(
        mixed, attention_full[4], preferred_element_type=jnp.float32
    ) + attention_full[5].astype(jnp.float32)
    normed_two, normalized_two, inverse_two, expanded = feedforward_inputs(rows, feedforward_full)
    activated = jax.nn.gelu(expanded, approximate=False).astype(jnp.bfloat16)
    shrunk = jnp.dot(
        activated, feedforward_full[4], preferred_element_type=jnp.float32
    ) + feedforward_full[5].astype(jnp.float32)
    layer_output = (rows + live_rows * (attended + shrunk)).astype(jnp.bfloat16)
    seed_rows = cotangent.astype(jnp.float32)
    branch_grad = (live_rows * seed_rows).astype(jnp.bfloat16)
    branch_total = jnp.sum(branch_grad.astype(jnp.float32), 0)
    feedforward_back = lax.all_gather(
        as_sent(lax.optimization_barrier((feedforward_parts, layer_output))[0]),
        "fsdp",
        axis=0,
        tiled=True,
    )
    normed_two, normalized_two, inverse_two, expanded = feedforward_inputs(rows, feedforward_back)
    activated = jax.nn.gelu(expanded, approximate=False).astype(jnp.bfloat16)
    shrink_weight_grad = jnp.einsum(
        "tf,td->fd", activated, branch_grad, preferred_element_type=jnp.float32
    )
    activated_grad = jnp.einsum(
        "td,fd->tf", branch_grad, feedforward_back[4], preferred_element_type=jnp.float32
    )
    expanded_grad = (activated_grad * gelu_slope(expanded)).astype(jnp.bfloat16)
    expand_bias_grad = jnp.sum(expanded_grad.astype(jnp.float32), 0)
    expand_weight_grad = jnp.einsum(
        "td,tf->df", normed_two, expanded_grad, preferred_element_type=jnp.float32
    )
    normed_two_grad = jnp.einsum(
        "tf,df->td", expanded_grad, feedforward_back[2], preferred_element_type=jnp.float32
    )
    rows_grad_two, ff_gain_grad, ff_shift_grad = norm_back(
        normed_two_grad, normalized_two, inverse_two, feedforward_back[0]
    )
    ff_terms = (
        ff_gain_grad,
        ff_shift_grad,
        expand_weight_grad,
        expand_bias_grad,
        shrink_weight_grad,
        branch_total,
    )
    ff_parts = (
        lax.psum_scatter(ff_terms[0], "fsdp", scatter_dimension=0, tiled=True),
        lax.psum_scatter(ff_terms[1], "fsdp", scatter_dimension=0, tiled=True),
        lax.psum_scatter(ff_terms[2], "fsdp", scatter_dimension=0, tiled=True),
        lax.psum_scatter(ff_terms[3], "fsdp", scatter_dimension=0, tiled=True),
        lax.psum_scatter(ff_terms[4], "fsdp", scatter_dimension=0, tiled=True),
        lax.psum_scatter(ff_terms[5], "fsdp", scatter_dimension=0, tiled=True),
    )
    attention_back = lax.all_gather(
        as_sent(lax.optimization_barrier((attention_parts, layer_output))[0]),
        "fsdp",
        axis=0,
        tiled=True,
    )
    normed_one, normalized_one, inverse_one, queries, keys, values = attention_inputs(
        rows, attention_back, cosine, sine
    )
    scores = score_block(queries, keys, allowed)
    probs = jnp.exp(scores - log_total)
    probs_low = probs.astype(jnp.bfloat16)
    mixed = jnp.einsum("hts,shd->thd", probs_low, values, preferred_element_type=jnp.float32)
    mixed = mixed.reshape(length, D).astype(jnp.bfloat16)
    output_weight_grad = jnp.einsum(
        "td,te->de", mixed, branch_grad, preferred_element_type=jnp.float32
    )
    mixed_grad = jnp.einsum(
        "te,de->td", branch_grad, attention_back[4], preferred_element_type=jnp.float32
    )
    mixed_grad = mixed_grad.astype(jnp.bfloat16).reshape(length, HEADS, HEAD_DIM)
    value_grad = jnp.einsum(
        "hts,thd->shd", probs_low, mixed_grad, preferred_element_type=jnp.float32
    )
    probs_grad = jnp.einsum("thd,shd->hts", mixed_grad, values, preferred_element_type=jnp.float32)
    scores_grad = (probs * (probs_grad - jnp.sum(probs_grad * probs, -1, keepdims=True))).astype(
        jnp.bfloat16
    )
    query_grad = jnp.einsum(
        "hts,shd->thd", scores_grad, keys, preferred_element_type=jnp.float32
    ) * HEAD_DIM ** (-0.5)
    key_grad = jnp.einsum(
        "hts,thd->shd", scores_grad, queries, preferred_element_type=jnp.float32
    ) * HEAD_DIM ** (-0.5)
    query_grad = turn(query_grad, cosine, sine, -1.0)
    key_grad = turn(key_grad, cosine, sine, -1.0)
    joined_grad = jnp.concatenate(
        [query_grad.reshape(length, D), key_grad.reshape(length, D), value_grad.reshape(length, D)],
        1,
    ).astype(jnp.bfloat16)
    joined_bias_grad = jnp.sum(joined_grad.astype(jnp.float32), 0)
    joined_weight_grad = jnp.einsum(
        "td,te->de", normed_one, joined_grad, preferred_element_type=jnp.float32
    )
    normed_one_grad = jnp.einsum(
        "te,de->td", joined_grad, attention_back[2], preferred_element_type=jnp.float32
    )
    rows_grad_one, at_gain_grad, at_shift_grad = norm_back(
        normed_one_grad, normalized_one, inverse_one, attention_back[0]
    )
    at_terms = (
        at_gain_grad,
        at_shift_grad,
        joined_weight_grad,
        joined_bias_grad,
        output_weight_grad,
        branch_total,
    )
    at_parts = (
        lax.psum_scatter(at_terms[0], "fsdp", scatter_dimension=0, tiled=True),
        lax.psum_scatter(at_terms[1], "fsdp", scatter_dimension=0, tiled=True),
        lax.psum_scatter(at_terms[2], "fsdp", scatter_dimension=0, tiled=True),
        lax.psum_scatter(at_terms[3], "fsdp", scatter_dimension=0, tiled=True),
        lax.psum_scatter(at_terms[4], "fsdp", scatter_dimension=0, tiled=True),
        lax.psum_scatter(at_terms[5], "fsdp", scatter_dimension=0, tiled=True),
    )
    input_grad = (seed_rows + rows_grad_one + rows_grad_two).astype(jnp.bfloat16)
    summed = (
        lax.psum(at_parts[0].astype(jnp.bfloat16), "rep").astype(jnp.float32),
        lax.psum(at_parts[1].astype(jnp.bfloat16), "rep").astype(jnp.float32),
        lax.psum(at_parts[2].astype(jnp.bfloat16), "rep").astype(jnp.float32),
        lax.psum(at_parts[3].astype(jnp.bfloat16), "rep").astype(jnp.float32),
        lax.psum(at_parts[4].astype(jnp.bfloat16), "rep").astype(jnp.float32),
        lax.psum(at_parts[5].astype(jnp.bfloat16), "rep").astype(jnp.float32),
        lax.psum(ff_parts[0].astype(jnp.bfloat16), "rep").astype(jnp.float32),
        lax.psum(ff_parts[1].astype(jnp.bfloat16), "rep").astype(jnp.float32),
        lax.psum(ff_parts[2].astype(jnp.bfloat16), "rep").astype(jnp.float32),
        lax.psum(ff_parts[3].astype(jnp.bfloat16), "rep").astype(jnp.float32),
        lax.psum(ff_parts[4].astype(jnp.bfloat16), "rep").astype(jnp.float32),
        lax.psum(ff_parts[5].astype(jnp.bfloat16), "rep").astype(jnp.float32),
    )
    return (
        layer_output,
        input_grad,
        summed[0],
        summed[1],
        summed[2],
        summed[3],
        summed[4],
        summed[5],
        summed[6],
        summed[7],
        summed[8],
        summed[9],
        summed[10],
        summed[11],
    )


def solution(mesh):
    placed = (
        P(("rep", "fsdp"), None),
        P(("rep", "fsdp"), None),
        P(("rep", "fsdp"), None),
        P("fsdp"),
        P("fsdp"),
        P("fsdp", None),
        P("fsdp"),
        P("fsdp", None),
        P("fsdp"),
        P("fsdp"),
        P("fsdp"),
        P("fsdp", None),
        P("fsdp"),
        P("fsdp", None),
        P("fsdp"),
        P(("rep", "fsdp"), None),
    )
    return jax.shard_map(
        body,
        mesh=mesh,
        in_specs=placed,
        out_specs=(
            P(("rep", "fsdp"), None),
            P(("rep", "fsdp"), None),
            P("fsdp"),
            P("fsdp"),
            P("fsdp", None),
            P("fsdp"),
            P("fsdp", None),
            P("fsdp"),
            P("fsdp"),
            P("fsdp"),
            P("fsdp", None),
            P("fsdp"),
            P("fsdp", None),
            P("fsdp"),
        ),
        check_vma=False,
    )
```

profile of v0, /device:TPU:10, one launch (start us, length us, event | category | flops | bytes accessed | tf_op | source)
XLA Modules:
  0.0 3220.2 jit_solution(5356058220467071223)
XLA Ops:
  10.2 19.3 all-gather.2
  29.5 18.0 all-gather.1
  47.5 19.3 all-gather
  67.4 18.0 all-gather.3
  85.4 19.5 all-gather.6
  105.0 18.0 all-gather.7
  123.0 19.1 all-gather.5
  142.1 17.8 all-gather.4
  160.6 10.2 fusion.93
  174.2 1.2 copy.124
  178.5 37.9 %all-gather.25.cloned.1.call-done = bf16[2048,2048]{1,0:T(8,128)(2,1)} async-done(((bf16[128,2048]{1,0:T(8,128)(2,1)}), bf16[2048,2048]{1,0:T(8,128)(2,1)}) %all-gather.25.cloned.1.call-update) | async-done | bytes 8388624 | tf_op jit(solution)/shard_map/all_gather | solution.py:151
  216.4 4.7 convolution_add_fusion.5
  221.1 163.8 %all-gather.29.cloned.1.call-done = bf16[8192,2048]{1,0:T(8,128)(2,1)} async-done(((bf16[512,2048]{1,0:T(8,128)(2,1)}), bf16[8192,2048]{1,0:T(8,128)(2,1)}) %all-gather.29.cloned.1.call-update) | async-done | bytes 33554448 | tf_op jit(solution)/shard_map/all_gather | solution.py:159
  384.9 169.5 %all-gather.27.cloned.1.call-done = bf16[2048,8192]{1,0:T(8,128)(2,1)} async-done(((bf16[128,8192]{1,0:T(8,128)(2,1)}), bf16[2048,8192]{1,0:T(8,128)(2,1)}) %all-gather.27.cloned.1.call-update) | async-done | bytes 33554448 | tf_op jit(solution)/shard_map/all_gather | solution.py:157
  554.4 27.7 fusion.28
  584.3 18.1 all-gather.8
  602.4 18.1 all-gather.10
  620.5 19.3 all-gather.9
  639.9 71.1 %all-gather.31.cloned.1.call-done = bf16[2048,6144]{1,0:T(8,128)(2,1)} async-done(((bf16[128,6144]{1,0:T(8,128)(2,1)}), bf16[2048,6144]{1,0:T(8,128)(2,1)}) %all-gather.31.cloned.1.call-update) | async-done | bytes 25165840 | tf_op jit(solution)/shard_map/all_gather | solution.py:226
  710.9 13.4 convolution_add_fusion.2
  724.3 3.5 copy.93
  727.9 2.1 slice.121
  730.0 2.7 fusion.243
  734.0 1.6 copy.125
  736.6 1.3 copy.127
  739.5 1.2 fusion.99
  741.2 9.0 fusion.239
  750.2 8.8 reduce-scatter.5.cloned.1.call-start
  759.1 28.2 all-gather.33.cloned.1.call-done
  787.3 7.1 convolution_convert_fusion
  794.4 1.5 copy.123
  800.8 1.3 pad_maximum_fusion.4
  802.1 1.3 copy.106
  803.4 2.3 pad_maximum_fusion.3
  805.7 1.3 copy.102
  807.0 1.7 convolution_convert_fusion.2
  808.8 21.8 fusion.234
  830.6 17.7 all-gather.13
  848.4 18.0 all-gather.12
  866.5 19.3 all-gather.11
  885.8 70.2 %all-gather.37.cloned.1.call-done = bf16[2048,8192]{1,0:T(8,128)(2,1)} async-done(((bf16[128,8192]{1,0:T(8,128)(2,1)}), bf16[2048,8192]{1,0:T(8,128)(2,1)}) %all-gather.37.cloned.1.call-update) | async-done | bytes 33554448 | tf_op jit(solution)/shard_map/all_gather | solution.py:185
  956.0 18.6 convolution_add_fusion
  974.6 151.3 %all-gather.35.cloned.1.call-done = bf16[8192,2048]{1,0:T(8,128)(2,1)} async-done(((bf16[512,2048]{1,0:T(8,128)(2,1)}), bf16[8192,2048]{1,0:T(8,128)(2,1)}) %all-gather.35.cloned.1.call-update) | async-done | bytes 33554448 | tf_op jit(solution)/shard_map/all_gather | solution.py:185
  1125.9 18.9 convert_reduce_fusion
  1144.8 28.2 fusion.231
  1173.3 29.9 fusion.29
  1203.2 103.1 %reduce-scatter.7.cloned.1.call-done = f32[128,2048]{1,0:T(8,128)} async-done(((f32[2048,2048]{1,0:T(8,128)}), f32[128,2048]{1,0:T(8,128)}) %reduce-scatter.7.cloned.1.call-update) | async-done | bytes 1048592 | tf_op jit(solution)/shard_map/reduce_scatter | solution.py:289
  1306.4 2.1 convert_element_type.270
  1308.4 466.2 %reduce-scatter.5.cloned.1.call-done = f32[128,6144]{1,0:T(8,128)} async-done(((f32[2048,6144]{1,0:T(8,128)}), f32[128,6144]{1,0:T(8,128)}) %reduce-scatter.5.cloned.1.call-update) | async-done | bytes 3145744 | tf_op jit(solution)/shard_map/reduce_scatter | solution.py:287
  1774.6 3.2 convert_element_type.262
  1777.8 633.3 %reduce-scatter.9.cloned.1.call-done = f32[128,8192]{1,0:T(8,128)} async-done(((f32[2048,8192]{1,0:T(8,128)}), f32[128,8192]{1,0:T(8,128)}) %reduce-scatter.9.cloned.1.call-update) | async-done | bytes 4194320 | tf_op jit(solution)/shard_map/reduce_scatter | solution.py:221
  2411.1 3.8 convert_element_type.279
  2414.9 631.8 %reduce-scatter.11.cloned.1.call-done = f32[512,2048]{1,0:T(8,128)} async-done(((f32[8192,2048]{1,0:T(8,128)}), f32[512,2048]{1,0:T(8,128)}) %reduce-scatter.11.cloned.1.call-update) | async-done | bytes 4194320 | tf_op jit(solution)/shard_map/reduce_scatter | solution.py:223
  3046.7 3.8 convert_element_type.285
  3053.7 1.7 convert_reduce_fusion.1
  3055.4 18.2 fusion.246
  3073.6 15.2 fusion.128
  3088.8 2.8 convert_reduce_fusion.3
  3091.7 53.5 %all-reduce.7 = (bf16[2048]{0:T(1024)(128)(2,1)S(1)}, bf16[2048]{0:T(1024)(128)(2,1)S(1)}, bf16[6144]{0:T(1024)(128)(2,1)S(1)}, bf16[2048]{0:T(1024)(128)(2,1)S(...) all-reduce(f32[2048]{0:T(1024)S(1)} %get-tuple-element.36, ...), channel_id=2, replica_groups=mesh['rep'=2,'fsdp'=16] {'fsdp'}, use_global_device_ids=true, to_apply=%region_11.12.clone | all-reduce | flops 24576 | bytes 147456
  3145.7 5.3 all-reduce.8
  3154.2 49.2 %all-reduce.12.cloned.1.call-done = (bf16[128,6144]{1,0:T(8,128)(2,1)}, bf16[128,2048]{1,0:T(8,128)(2,1)}, bf16[128,8192]{1,0:T(8,128)(2,1)}, bf16[512,2048]{1,0:T(8,128)(2,1)}) async-done(((bf16[128,6144]{1,0:T(8,128)(2,1)}, bf16[128,2048]{1,0:T(8,128)(2,1)}, bf16[128,8192]{1,0:T(8,128)(2,1)}, bf16[512,2048]{1,0:T(8,128)(2,1)}), (bf16[128,6144]{1,0:T(8,128)(2,1)}, bf16[128,2048]{1,0:T(8,128)(2,1)}, ...) | async-done | bytes 6291472 | tf_op jit(solution)/shard_map/psum | solution.py:296
  3203.4 3.5 convert_element_type.263
  3208.0 2.4 convert_element_type.280
  3210.4 2.5 convert_element_type.286
  (175 shorter events, 28.7 us)
Async XLA Ops:
  7.2 3.0 copy-start.26
  7.2 22.3 copy-start.29
  7.2 40.3 %copy-start.28 = (bf16[128]{0:T(256)(128)(2,1)S(1)}, bf16[128]{0:T(256)(128)(2,1)}, u32[]{:S(2)}) copy-start(bf16[128]{0:T(256)(128)(2,1)} %param.19) | copy-start | bytes 772
  7.2 59.7 %copy-start.27 = (s32[1,128]{1,0:T(1,128)S(1)}, s32[1,128]{1,0:T(1,128)}, u32[]{:S(2)}) copy-start(s32[1,128]{1,0:T(1,128)} %param.17) | copy-start | bytes 1540
  7.2 60.1 %copy-start.32 = (bf16[128]{0:T(256)(128)(2,1)S(1)}, bf16[128]{0:T(256)(128)(2,1)}, u32[]{:S(2)}) copy-start(bf16[128]{0:T(256)(128)(2,1)} %param.24) | copy-start | bytes 772
  7.2 78.2 %copy-start.25 = (bf16[512]{0:T(512)(128)(2,1)S(1)}, bf16[512]{0:T(512)(128)(2,1)}, u32[]{:S(2)}) copy-start(bf16[512]{0:T(512)(128)(2,1)} %param.28) | copy-start | bytes 3076
  7.2 97.8 %copy-start.33 = (bf16[128]{0:T(256)(128)(2,1)S(1)}, bf16[128]{0:T(256)(128)(2,1)}, u32[]{:S(2)}) copy-start(bf16[128]{0:T(256)(128)(2,1)} %param.30) | copy-start | bytes 772
  7.3 115.8 %copy-start.30 = (bf16[128]{0:T(256)(128)(2,1)S(1)}, bf16[128]{0:T(256)(128)(2,1)}, u32[]{:S(2)}) copy-start(bf16[128]{0:T(256)(128)(2,1)} %param.26) | copy-start | bytes 772
  7.3 134.9 %copy-start.31 = (bf16[128]{0:T(256)(128)(2,1)S(1)}, bf16[128]{0:T(256)(128)(2,1)}, u32[]{:S(2)}) copy-start(bf16[128]{0:T(256)(128)(2,1)} %param.25) | copy-start | bytes 772
  7.3 152.7 %copy-start = (bf16[128,2048]{1,0:T(8,128)(2,1)S(1)}, bf16[128,2048]{1,0:T(8,128)(2,1)}, u32[]{:S(2)}) copy-start(bf16[128,2048]{1,0:T(8,128)(2,1)} %param.16) | copy-start | bytes 1572868
  7.3 153.1 %copy-start.34 = (s32[1,128]{1,0:T(1,128)S(1)}, s32[1,128]{1,0:T(1,128)}, u32[]{:S(2)}) copy-start(s32[1,128]{1,0:T(1,128)} %param.18) | copy-start | bytes 1540
  7.3 153.3 %all-gather.23.cloned.1.call-start = ((), (), s32[]{:S(2)}) async-start(), calls=%async_computation.4 | async-start | bytes 26738688 | tf_op jit(solution)/shard_map/all_gather | solution.py:149
  8.0 208.4 %all-gather.25.cloned.1.call-start = ((), (), s32[]{:S(2)}) async-start(), calls=%async_computation.5 | async-start | bytes 8912896 | tf_op jit(solution)/shard_map/all_gather | solution.py:151
  8.8 376.2 %all-gather.29.cloned.1.call-start = ((), (), s32[]{:S(2)}) async-start(), calls=%async_computation.7 | async-start | bytes 35651584 | tf_op jit(solution)/shard_map/all_gather | solution.py:159
  9.5 544.9 %all-gather.27.cloned.1.call-start = ((), (), s32[]{:S(2)}) async-start(), calls=%async_computation.6 | async-start | bytes 35651584 | tf_op jit(solution)/shard_map/all_gather | solution.py:157
  10.1 700.9 %all-gather.31.cloned.1.call-start = ((), (), s32[]{:S(2)}) async-start(), calls=%async_computation.8 | async-start | bytes 26738688 | tf_op jit(solution)/shard_map/all_gather | solution.py:226
  175.4 1.1 copy-start.21
  175.4 1.4 copy-start.22
  176.2 2.0 copy-start.24
  582.1 205.2 %all-gather.33.cloned.1.call-start = ((), (), s32[]{:S(2)}) async-start(), calls=%async_computation.9 | async-start | bytes 8912896 | tf_op jit(solution)/shard_map/all_gather | solution.py:226
  582.7 373.3 %all-gather.37.cloned.1.call-start = ((), (), s32[]{:S(2)}) async-start(), calls=%async_computation.11 | async-start | bytes 35651584 | tf_op jit(solution)/shard_map/all_gather | solution.py:185
  583.5 542.4 %all-gather.35.cloned.1.call-start = ((), (), s32[]{:S(2)}) async-start(), calls=%async_computation.10 | async-start | bytes 35651584 | tf_op jit(solution)/shard_map/all_gather | solution.py:185
  584.2 722.2 %reduce-scatter.7.cloned.1.call-start = ((), (), s32[]{:S(2)}) async-start(), calls=%async_computation.13 | async-start | bytes 17825792 | tf_op jit(solution)/shard_map/reduce_scatter | solution.py:289
  737.9 1.6 copy-start.14
  737.9 1.6 copy-start.16
  738.7 0.8 copy-start.6
  738.7 2.0 copy-start.8
  738.8 2.4 copy-start.10
  738.8 2.4 copy-start.12
  738.8 2.4 copy-start.3
  750.2 1024.4 %reduce-scatter.5.cloned.1.call-start = ((), (), s32[]{:S(2)}) async-start(), calls=%async_computation.12 | async-start | bytes 53477376 | tf_op jit(solution)/shard_map/reduce_scatter | solution.py:287
  794.4 2.1 copy-start.11
  795.9 2.2 copy-start.5
  795.9 1.3 copy-start.13
  795.9 1.5 copy-start.17
  796.2 2.0 copy-start.7
  796.3 2.0 copy-start.9
  796.3 2.0 copy-start.15
  807.0 23.5 copy-start.1
  808.8 21.8 copy-start.2
  830.6 1580.5 %reduce-scatter.9.cloned.1.call-start = ((), (), s32[]{:S(2)}) async-start(), calls=%async_computation.14 | async-start | bytes 71303168 | tf_op jit(solution)/shard_map/reduce_scatter | solution.py:221
  1173.1 1873.6 %reduce-scatter.11.cloned.1.call-start = ((), (), s32[]{:S(2)}) async-start(), calls=%async_computation.15 | async-start | bytes 71303168 | tf_op jit(solution)/shard_map/reduce_scatter | solution.py:223
  1203.2 2000.2 %all-reduce.12.cloned.1.call-start = ((), (), s32[]{:S(2)}) async-start(), calls=%async_computation.16 | async-start | bytes 12582912 | tf_op jit(solution)/shard_map/psum | solution.py:296
  3050.5 0.7 copy-start.35
  3073.6 15.2 copy-start.4
  3073.6 15.2 copy-start.18
  3152.6 60.4 %copy-start.36 = (f32[128]{0:T(128)}, f32[128]{0:T(128)S(1)}, u32[]{:S(2)}) copy-start(f32[128]{0:T(128)S(1)} %convert_element_type.274) | copy-start | bytes 1540
  3203.4 3.5 copy-start.23
  3203.4 4.6 copy-start.20
  3206.9 3.5 copy-start.19
Sparse Core Ops, SparseCore 0:
  9.7 129.9 all-gather.22
  141.9 74.5 all-gather.24
  218.0 166.8 all-gather.28
  386.4 168.0 all-gather.26
  582.2 128.6 all-gather.30
  713.0 74.2 all-gather.32
  788.9 167.0 all-gather.36
  957.6 168.2 all-gather.34
  1130.0 176.2 reduce-scatter.6
  1310.4 464.1 reduce-scatter.4
  1778.9 632.2 reduce-scatter.8
  2415.2 631.4 reduce-scatter.10
  3050.7 152.6 all-reduce.11
where the time goes:
time: 3240 us; the launch traced here: 3220 us
  waiting for transfers between devices  2580 us (80%)
  blocking collectives  318 us (10%)
  matrix products  229 us (7%)
  other arithmetic  37.4 us (1%)
    reduce_scatter x1, waiting for transfers between devices, body(): lax.psum_scatter(ff_terms[2], 'fsdp', scatter_dimension=0, tiled=True)  633 us
    reduce_scatter x1, waiting for transfers between devices, body(): lax.psum_scatter(ff_terms[4], 'fsdp', scatter_dimension=0, tiled=True)  632 us
    reduce_scatter x1, waiting for transfers between devices, body(): lax.psum_scatter(at_terms[2], 'fsdp', scatter_dimension=0, tiled=True)  466 us
    all_gather x2, waiting for transfers between devices, body(): lax.all_gather(as_sent(lax.optimization_barrier((feedforward_parts, layer...  222 us
    all_gather x1, waiting for transfers between devices, body(): lax.all_gather(expand_weight, 'fsdp', axis=0, tiled=True)  170 us
    all_gather x1, waiting for transfers between devices, body(): lax.all_gather(shrink_weight, 'fsdp', axis=0, tiled=True)  164 us
    reduce_scatter x1, waiting for transfers between devices, body(): lax.psum_scatter(at_terms[4], 'fsdp', scatter_dimension=0, tiled=True)  103 us
    all_gather x2, waiting for transfers between devices, body(): lax.all_gather(as_sent(lax.optimization_barrier((attention_parts, layer_o...  99.2 us
  transfers between devices with their start and end apart: 13, of which 12 were waited for; matrix products, arithmetic and copies ran while one was open for 8% of the time, Pallas kernels for 0%

commit v1 on v0

--- a/solution.py
+++ b/solution.py
@@ -1,3 +1,5 @@
+import functools
+
 import jax
 import jax.numpy as jnp
 from jax import lax
@@ -322,7 +324,217 @@
     )
 
 
+def wide(a):
+    return a.astype(jnp.float32)
+
+
+def normalize(rows):
+    centre = jnp.mean(rows, -1, keepdims=True)
+    centred = rows - centre
+    inverse = lax.rsqrt(jnp.mean(centred * centred, -1, keepdims=True) + epsilon)
+    return (centred * inverse, inverse)
+
+
+def head_body(
+    n,
+    layer_input,
+    segment,
+    live_mask,
+    attention_gain,
+    attention_shift,
+    joined_weight,
+    joined_bias,
+    output_weight,
+    output_bias,
+    feedforward_gain,
+    feedforward_shift,
+    expand_weight,
+    expand_bias,
+    shrink_weight,
+    shrink_bias,
+    cotangent,
+):
+    me = lax.axis_index("fsdp")
+    own = layer_input.shape[0]
+    width = layer_input.shape[1]
+    part = width // n
+    third = joined_bias.shape[0]
+    piece = expand_weight.shape[1] // n
+    heads = HEADS // n
+    cols = heads * HEAD_DIM
+    tokens = own * n
+    low = jnp.bfloat16
+    live_rows = wide(live_mask[0])[:, None]
+    seeds = wide(cotangent)
+    branch_own = (live_rows * seeds).astype(low)
+    small = jnp.concatenate(
+        [
+            attention_gain,
+            attention_shift,
+            feedforward_gain,
+            feedforward_shift,
+            output_bias,
+            shrink_bias,
+            joined_bias,
+            segment[0].astype(low),
+        ]
+    )
+    small = jnp.pad(small, (0, -small.shape[0] % width)).reshape(-1, width)
+    extra = small.shape[0]
+    rows_all = lax.all_gather(jnp.concatenate([layer_input, small], 0), "fsdp", axis=0)
+    small_all = rows_all[:, own:].reshape(n, extra * width)
+    rows = wide(rows_all[:, :own]).reshape(tokens, width)
+    branch = lax.all_gather(branch_own, "fsdp", axis=0, tiled=True)
+    gain_one, shift_one, gain_two, shift_two, bias_o, bias_s = (
+        wide(small_all[:, k * part : (k + 1) * part]).reshape(width) for k in range(6)
+    )
+    bias_j = wide(small_all[:, 6 * part : 6 * part + third]).reshape(3, n, cols)
+    bias_j = lax.dynamic_index_in_dim(bias_j, me, 1, keepdims=False).reshape(3 * cols)
+    seg_all = small_all[:, 6 * part + third : 6 * part + third + own]
+
+    sent = jnp.concatenate(
+        [
+            joined_weight.reshape(part, 3, n, cols).transpose(2, 0, 1, 3).reshape(n, part, 3 * cols),
+            expand_weight.reshape(part, n, piece).transpose(1, 0, 2),
+        ],
+        2,
+    )
+    held = lax.all_to_all(sent, "fsdp", 0, 0).reshape(width, 3 * cols + piece)
+    weight_j, weight_e = (held[:, : 3 * cols], held[:, 3 * cols :])
+    weight_os = jnp.concatenate([output_weight, shrink_weight], 0)
+
+    normalized, inverse = normalize(rows)
+    normed_one = (normalized * gain_one + shift_one).astype(low)
+    normed_two = (normalized * gain_two + shift_two).astype(low)
+    joined = jnp.dot(normed_one, weight_j, preferred_element_type=jnp.float32) + bias_j
+    seg_int = seg_all.astype(jnp.int32)
+    cosine, sine = rotary_tables(seg_int)
+    places = jnp.arange(own, dtype=jnp.int32)
+    allowed = (seg_int[:, :, None] == seg_int[:, None, :]) & (
+        places[None, None, :] <= places[None, :, None]
+    )
+    split = joined.reshape(n, own, 3, heads, HEAD_DIM)
+    queries = turn(split[:, :, 0], cosine, sine, 1.0).astype(low)
+    keys = turn(split[:, :, 1], cosine, sine, 1.0).astype(low)
+    values = split[:, :, 2].astype(low)
+    scale = HEAD_DIM ** (-0.5)
+    scores = (
+        jnp.einsum("bthd,bshd->bhts", queries, keys, preferred_element_type=jnp.float32) * scale
+    )
+    scores = jnp.where(allowed[:, None], scores, masked_score)
+    top = jnp.max(scores, -1, keepdims=True)
+    expo = jnp.exp(scores - top)
+    probs = expo / jnp.sum(expo, -1, keepdims=True)
+    probs_low = probs.astype(low)
+    mixed = jnp.einsum("bhts,bshd->bthd", probs_low, values, preferred_element_type=jnp.float32)
+    mixed = mixed.reshape(tokens, cols).astype(low)
+    expanded = jnp.dot(normed_two, weight_e, preferred_element_type=jnp.float32) + wide(expand_bias)
+    activated = jax.nn.gelu(expanded, approximate=False).astype(low)
+    slope = gelu_slope(expanded)
+    inner = jnp.concatenate([mixed, activated], 1)
+    partial = jnp.dot(inner, weight_os, preferred_element_type=jnp.float32).astype(low)
+    summed = lax.psum_scatter(partial, "fsdp", scatter_dimension=0, tiled=True)
+    layer_output = (
+        wide(layer_input) + live_rows * (wide(summed) + (bias_o + bias_s))
+    ).astype(low)
+
+    grad_os = jnp.einsum("tf,td->fd", inner, branch, preferred_element_type=jnp.float32)
+    inner_grad = jnp.einsum("td,fd->tf", branch, weight_os, preferred_element_type=jnp.float32)
+    expanded_grad = (inner_grad[:, cols:] * slope).astype(low)
+    mixed_grad = inner_grad[:, :cols].astype(low).reshape(n, own, heads, HEAD_DIM)
+    value_grad = jnp.einsum(
+        "bhts,bthd->bshd", probs_low, mixed_grad, preferred_element_type=jnp.float32
+    )
+    probs_grad = jnp.einsum(
+        "bthd,bshd->bhts", mixed_grad, values, preferred_element_type=jnp.float32
+    )
+    scores_grad = (probs * (probs_grad - jnp.sum(probs_grad * probs, -1, keepdims=True))).astype(low)
+    query_grad = (
+        jnp.einsum("bhts,bshd->bthd", scores_grad, keys, preferred_element_type=jnp.float32) * scale
+    )
+    key_grad = (
+        jnp.einsum("bhts,bthd->bshd", scores_grad, queries, preferred_element_type=jnp.float32)
+        * scale
+    )
+    query_grad = turn(query_grad, cosine, sine, -1.0)
+    key_grad = turn(key_grad, cosine, sine, -1.0)
+    joined_grad = jnp.concatenate(
+        [a.reshape(tokens, cols) for a in (query_grad, key_grad, value_grad)], 1
+    ).astype(low)
+    grad_j = jnp.einsum("td,te->de", normed_one, joined_grad, preferred_element_type=jnp.float32)
+    grad_e = jnp.einsum("td,tf->df", normed_two, expanded_grad, preferred_element_type=jnp.float32)
+    back_one = jnp.einsum("te,de->td", joined_grad, weight_j, preferred_element_type=jnp.float32)
+    back_two = jnp.einsum("tf,df->td", expanded_grad, weight_e, preferred_element_type=jnp.float32)
+    hat = (back_one * gain_one + back_two * gain_two).astype(low)
+    hat_own = wide(lax.psum_scatter(hat, "fsdp", scatter_dimension=0, tiled=True))
+    rows_own = wide(layer_input)
+    normalized_own, inverse_own = normalize(rows_own)
+    row_grad = inverse_own * (
+        hat_own
+        - jnp.mean(hat_own, -1, keepdims=True)
+        - normalized_own * jnp.mean(hat_own * normalized_own, -1, keepdims=True)
+    )
+    input_grad = (seeds + row_grad).astype(low)
+
+    grads = jnp.concatenate([grad_j, grad_e], 1).astype(low).reshape(n, part, 3 * cols + piece)
+    grads = lax.all_to_all(grads, "fsdp", 0, 0)
+    joined_weight_grad = (
+        grads[:, :, : 3 * cols].reshape(n, part, 3, cols).transpose(1, 2, 0, 3).reshape(part, 3 * width)
+    )
+    expand_weight_grad = grads[:, :, 3 * cols :].transpose(1, 0, 2).reshape(part, n * piece)
+
+    vectors = jnp.stack(
+        [
+            jnp.sum(back_one * normalized, 0),
+            jnp.sum(back_one, 0),
+            jnp.sum(back_two * normalized, 0),
+            jnp.sum(back_two, 0),
+        ]
+    )
+    bias_j_grad = jnp.sum(wide(joined_grad), 0).reshape(3, 1, cols)
+    bias_j_grad = jnp.where(
+        lax.broadcasted_iota(jnp.int32, (3, n, cols), 1) == me, bias_j_grad, 0.0
+    ).reshape(-1)
+    branch_sum = jnp.sum(wide(branch_own), 0)
+    small_sums = lax.psum(
+        jnp.concatenate([vectors.reshape(-1), branch_sum, bias_j_grad]), ("rep", "fsdp")
+    )
+    pieces = small_sums[: 5 * width].reshape(5, n, part)
+    pieces = lax.dynamic_index_in_dim(pieces, me, 1, keepdims=False)
+    joined_bias_grad = lax.dynamic_slice(small_sums, (5 * width + me * third,), (third,))
+    expand_bias_grad = jnp.sum(wide(expanded_grad), 0)
+    rest = lax.psum(
+        (
+            joined_weight_grad,
+            expand_weight_grad,
+            grad_os[:cols].astype(low),
+            grad_os[cols:].astype(low),
+            expand_bias_grad.astype(low),
+        ),
+        "rep",
+    )
+    rest = tuple(wide(a) for a in rest)
+    return (
+        layer_output,
+        input_grad,
+        pieces[0],
+        pieces[1],
+        rest[0],
+        joined_bias_grad,
+        rest[2],
+        pieces[4],
+        pieces[2],
+        pieces[3],
+        rest[1],
+        rest[4],
+        rest[3],
+        pieces[4],
+    )
+
+
 def solution(mesh):
+    n = mesh.shape["fsdp"]
+    chosen = functools.partial(head_body, n) if HEADS % n == 0 else body
     placed = (
         P(("rep", "fsdp"), None),
         P(("rep", "fsdp"), None),
@@ -342,7 +554,7 @@
         P(("rep", "fsdp"), None),
     )
     return jax.shard_map(
-        body,
+        chosen,
         mesh=mesh,
         in_specs=placed,
         out_specs=(

time: 3240 us -> 841 us (0.26)
  waiting for transfers between devices: 2580 us -> 580 us
  blocking collectives: 318 us -> 4.94 us
  matrix products: 229 us -> 88.4 us
  local copies, waits for them, and re-layouts: 28.6 us -> 81.3 us
    reduce_scatter x4 -> x2, waiting for transfers between devices: 1830 us -> 191 us  [the longest x1 106 us: head_body(): summed = lax.psum_scatter(partial, 'fsdp', scatter_dimension=0, tiled=True)]
    all_gather x8 -> x2, waiting for transfers between devices: 692 us -> 52 us  [the longest x1 52 us: head_body(): lax.all_gather(jnp.concatenate([layer_input, small], 0), 'fsdp', axis=0)]
    all_gather x14 -> x0, blocking collectives: 260 us -> none  [the longest x3 55.6 us: body(): lax.all_gather(as_sent(lax.optimization_barrier((attention_parts, layer_o...]
    all_to_all x0 -> x2, waiting for transfers between devices: none -> 183 us  [the longest x1 113 us: head_body(): held = lax.all_to_all(sent, 'fsdp', 0, 0).reshape(width, 3 * cols + piece)]
    dot_general x21 -> x14, matrix products: 229 us -> 87.2 us  [the longest x1 14.9 us: head_body(): jnp.einsum('te,de->td', joined_grad, weight_j, preferred_element_type=jnp...]
    psum x1 -> x2, waiting for transfers between devices: 49.2 us -> 153 us  [the longest x1 153 us: head_body(): lax.psum((joined_weight_grad, expand_weight_grad, grad_os[:cols].astype(l...]
    unnamed x1 -> x0, blocking collectives: 53.5 us -> none
  transfers between devices with their start and end apart: 13 -> 8, of which waited for: 12 -> 6; matrix products, arithmetic and copies ran while one was open for 8% -> 15% of each run, Pallas kernels for 0% -> 0%
where the time goes in v1:
time: 841 us; the launch traced here: 834 us
  waiting for transfers between devices  580 us (69%)
  matrix products  88.4 us (11%)
  local copies, waits for them, and re-layouts  81.3 us (10%)
  other arithmetic  52.2 us (6%)
  between operations  14.9 us (2%)
  starting transfers between devices  12.2 us (1%)
    psum x1, waiting for transfers between devices, head_body(): lax.psum((joined_weight_grad, expand_weight_grad, grad_os[:cols].astype(l...  153 us
    all_to_all x1, waiting for transfers between devices, head_body(): held = lax.all_to_all(sent, 'fsdp', 0, 0).reshape(width, 3 * cols + piece)  113 us
    reduce_scatter x1, waiting for transfers between devices, head_body(): summed = lax.psum_scatter(partial, 'fsdp', scatter_dimension=0, tiled=True)  106 us
    reduce_scatter x1, waiting for transfers between devices, head_body(): lax.psum_scatter(hat, 'fsdp', scatter_dimension=0, tiled=True)  85.8 us
    all_to_all x1, waiting for transfers between devices, head_body(): grads = lax.all_to_all(grads, 'fsdp', 0, 0)  69.5 us
    all_gather x1, waiting for transfers between devices, head_body(): lax.all_gather(jnp.concatenate([layer_input, small], 0), 'fsdp', axis=0)  52 us
    unnamed x65, local copies, waits for them, and re-layouts  28.1 us
  transfers between devices with their start and end apart: 8, of which 6 were waited for; matrix products, arithmetic and copies ran while one was open for 15% of the time, Pallas kernels for 0%

profile of v1, /device:TPU:10, one launch (start us, length us, event | category | flops | bytes accessed | tf_op | source)
XLA Modules:
  0.0 833.7 jit_solution(5947219598620714411)
XLA Ops:
  8.0 2.0 convert_reduce_fusion.4
  10.1 0.9 dynamic-update-slice.2
  11.0 0.8 dynamic-update-slice.3
  11.8 0.8 dynamic-update-slice.4
  12.6 0.8 dynamic-update-slice.5
  13.5 0.8 dynamic-update-slice.6
  14.3 0.8 dynamic-update-slice.7
  15.1 0.9 dynamic-update-slice.8
  16.9 1.9 maximum_bitcast_fusion
  18.8 0.9 copy.134
  19.7 1.2 copy.135
  20.9 3.3 copy.136
  24.2 3.6 pad_maximum_fusion
  27.8 6.5 all-to-all-start
  34.6 0.8 constant_dynamic-update-slice_fusion.1
  35.4 1.5 constant_dynamic-update-slice_fusion
  36.9 113.5 %all-to-all-done = bf16[16,128,896]{1,2,0:T(8,128)(2,1)} async-done(((bf16[16,128,896]{1,2,0:T(8,128)(2,1)}), bf16[16,128,896]{1,2,0:T(8,128)(2,1)}, u32[]{:S(2)}, u32[]{:S(2)}) %all-to-all-start) | async-done | bytes 3670048 | tf_op jit(solution)/shard_map/all_to_all | solution.py:402
  150.4 6.1 copy.137
  156.5 10.0 %fusion.119 = f32[2048,640]{1,0:T(8,128)S(1)} fusion(bf16[2048,2048]{1,0:T(8,128)(2,1)} %all-gather.5.cloned.1.call-done, bf16[640,2048]{1,0:T(8,128)(2,1)} %constant_dynamic-update-slice_fusion), kind=kOutput, calls=%fused_computation.205 | convolution fusion | flops 5368709120 | bytes 16252928 | tf_op jit(solution)/shard_map/td,fd->tf/dot_general | solution.py:442
  166.5 2.3 copy-done.15
  168.8 0.8 slice.288
  169.6 52.0 %all-gather.7.cloned.1.call-done = bf16[16,129,2048]{2,1,0:T(8,128)(2,1)} async-done(((bf16[1,129,2048]{2,1,0:T(8,128)(2,1)}), bf16[16,129,2048]{2,1,0:T(8,128)(2,1)}) %all-gather.7.cloned.1.call-update) | async-done | bytes 8454160 | tf_op jit(solution)/shard_map/all_gather | solution.py:384
  221.7 1.3 slice.181
  223.0 4.8 convert_reduce_fusion
  227.9 2.7 multiply_reduce_fusion.2
  230.7 9.7 %add_convert_fusion.2 = (bf16[2048,2048]{1,0:T(8,128)(2,1)S(1)}, bf16[2048,2048]{1,0:T(8,128)(2,1)}) fusion(f32[2048]{0:T(1024)S(1)} %get-tuple-element.118, f32[2048]{0:T(1024)S(1)} %get-tuple-element.119, f32[2048]{0:T(1024)S(1)} %rsqrt_bitcast_fusion, f32[2048]{0:T(1024)S(1)} %get-tuple-element.127, ...), kind=kLoop, calls=%fused_computation.7 | loop fusion | flops 37748736 | bytes 25214976 | tf_op jit(solution)/shard_map/convert_element_type | solution.py:407
  240.4 3.2 copy-done.1
  243.6 7.6 convolution_add_fusion
  251.2 2.8 copy.138
  257.3 1.1 fusion.118
  258.5 1.6 convolution_convert_fusion.4
  260.0 0.8 multiply_reduce_fusion.3
  264.4 11.0 %fusion.114 = (bf16[512]{0:T(512)(128)(2,1)S(1)}, bf16[2048,512]{1,0:T(8,128)(2,1)S(1)}, f32[2048,512]{1,0:T(8,128)}) fusion(f32[512]{0:T(512)S(1)} %convert_element_type.172, f32[2048,640]{1,0:T(8,128)} %copy-done.15, bf16[2048,2048]{1,0:T(8,128)(2,1)} %get-tuple-element.102, bf16[2048,896]{1,0:T(8,128)(2,1)} %bitcast.197), kind=kOutput, calls=%fused_computation.202 | convolution fusion | flops 4307549696 | bytes 20974592 | tf_op jit(solution)/shard_map/dot_general | solution.py:431
  275.4 8.4 %fusion.23 = f32[2048,2048]{1,0:T(8,128)} fusion(bf16[2048,512]{1,0:T(8,128)(2,1)S(1)} %get-tuple-element.97, bf16[2048,896]{1,0:T(8,128)(2,1)S(1)} %bitcast.198), kind=kOutput, calls=%fused_computation.47 | convolution fusion | flops 4294967296 | bytes 20971520 | tf_op jit(solution)/shard_map/tf,df->td/dot_general | solution.py:467
  284.3 14.9 %multiply_reduce_fusion.1 = (f32[2048]{0:T(1024)S(1)}, f32[2048]{0:T(1024)S(1)}, f32[2048]{0:T(1024)S(1)}, f32[2048]{0:T(1024)S(1)}, bf16[2048,2048]{1,0:T(8,128)(2,1)}) fusion(f32[2048]{0:T(1024)S(1)} %rsqrt_bitcast_fusion, f32[2048]{0:T(1024)S(1)} %get-tuple-element.127, bf16[16,129,2048]{2,1,0:T(8,128)(2,1)} %all-gather.7.cloned.1.call-done, ...), kind=kOutput, calls=%fused_computation.4 | convolution fusion | flops 3280461824 | bytes 36765696 | tf_op jit(solution)/shard_map/te,de->td/dot_general | solution.py:466
  301.5 1.9 copy-done.4
  303.4 9.4 %fusion.4 = bf16[2048,512]{1,0:T(8,128)(2,1)S(1)} fusion(f32[2048,512]{1,0:T(8,128)S(1)} %copy-done.4, f32[512]{0:T(512)S(1)} %convert_element_type.172), kind=kLoop, calls=%fused_computation.15 | loop fusion | flops 69206016 | bytes 6293504 | tf_op jit(solution)/shard_map/convert_element_type | solution.py:432
  312.8 10.7 %convolution_convert_fusion = bf16[2048,2048]{1,0:T(8,128)(2,1)} fusion(bf16[640,2048]{1,0:T(8,128)(2,1)} %constant_dynamic-update-slice_fusion, bf16[2048,512]{1,0:T(8,128)(2,1)S(1)} %fusion.4, bf16[2048,128]{1,0:T(8,128)(2,1)S(1)} %bitcast.223), kind=kOutput, calls=%fused_computation.10 | convolution fusion | flops 5378146304 | bytes 13631488 | tf_op jit(solution)/shard_map/dot_general | solution.py:435
  323.5 12.4 %copy.167 = bf16[2048,2048]{1,0:T(8,128)(2,1)} copy(bf16[2048,2048]{0,1:T(8,128)(2,1)} %bitcast.184) | data formatting | bytes 16777216 | tf_op jit(solution)/shard_map/td,tf->df/dot_general | solution.py:465
  335.9 12.3 %copy.166 = bf16[2048,2048]{1,0:T(8,128)(2,1)} copy(bf16[2048,2048]{0,1:T(8,128)(2,1)} %bitcast.183) | data formatting | bytes 16777216 | tf_op jit(solution)/shard_map/td,te->de/dot_general | solution.py:464
  348.2 8.1 convolution_convert_fusion.2
  356.4 4.7 fusion.20
  361.0 2.4 pad_maximum_fusion.1
  363.4 5.3 all-to-all-start.1
  368.8 8.3 convolution_convert_fusion.1
  377.1 0.8 slice.212
  377.9 1.5 slice.214
  379.3 69.5 %all-to-all-done.1 = bf16[16,128,896]{2,1,0:T(8,128)(2,1)} async-done(((bf16[16,128,896]{2,1,0:T(8,128)(2,1)}), bf16[16,128,896]{2,1,0:T(8,128)(2,1)}, u32[]{:S(2)}, u32[]{:S(2)}) %all-to-all-start.1) | async-done | bytes 3670048 | tf_op jit(solution)/shard_map/all_to_all | solution.py:480
  448.9 1.8 slice_bitcast_fusion
  450.7 2.4 copy.158
  453.0 1.7 slice.211
  454.7 1.0 copy.156
  455.7 1.2 copy.157
  457.4 4.9 psum.46
  464.3 1.4 dynamic_slice.13
  465.6 85.8 %reduce-scatter.5.cloned.1.call-done = bf16[128,2048]{1,0:T(8,128)(2,1)} async-done(((bf16[2048,2048]{1,0:T(8,128)(2,1)}), bf16[128,2048]{1,0:T(8,128)(2,1)}) %reduce-scatter.5.cloned.1.call-update) | async-done | bytes 524304 | tf_op jit(solution)/shard_map/reduce_scatter | solution.py:469
  551.4 1.4 convert_reduce_fusion.2
  552.9 105.6 %reduce-scatter.3.cloned.1.call-done = bf16[128,2048]{1,0:T(8,128)(2,1)} async-done(((bf16[2048,2048]{1,0:T(8,128)(2,1)}), bf16[128,2048]{1,0:T(8,128)(2,1)}) %reduce-scatter.3.cloned.1.call-update) | async-done | bytes 524304 | tf_op jit(solution)/shard_map/reduce_scatter | solution.py:436
  658.5 2.7 fusion.43
  661.2 152.7 %all-reduce.7.cloned.1.call-done = (bf16[128,6144]{0,1:T(8,128)(2,1)}, bf16[128,8192]{0,1:T(8,128)(2,1)}, bf16[128,2048]{1,0:T(8,128)(2,1)}, bf16[512,2048]{1,0:T(8,128)(2,1)}) async-done(((bf16[128,6144]{0,1:T(8,128)(2,1)}, bf16[128,8192]{0,1:T(8,128)(2,1)}, bf16[128,2048]{1,0:T(8,128)(2,1)}, bf16[512,2048]{1,0:T(8,128)(2,1)}), (bf16[128,6144]{0,1:T(8,128)(2,1)}, bf16[128,8192]{0,1:T(8,128)(2,1)}, ...) | async-done | bytes 6291472 | tf_op jit(solution)/shard_map/psum | solution.py:506
  813.9 2.1 convert_element_type.189
  816.1 3.1 copy.159
  819.1 4.4 copy.160
  823.6 2.5 convert_element_type.192
  (114 shorter events, 14.5 us)
Async XLA Ops:
  7.2 11.6 %copy-start.9 = (bf16[128,6144]{1,0:T(8,128)(2,1)S(1)}, bf16[128,6144]{1,0:T(8,128)(2,1)}, u32[]{:S(2)}) copy-start(bf16[128,6144]{1,0:T(8,128)(2,1)} %param.21) | copy-start | bytes 4718596
  7.2 149.3 %all-gather.5.cloned.1.call-start = ((), (), s32[]{:S(2)}) async-start(), calls=%async_computation.5 | async-start | bytes 8912896 | tf_op jit(solution)/shard_map/all_gather | solution.py:387
  8.0 2.0 copy-start.16
  10.1 211.6 %all-gather.7.cloned.1.call-start = ((), (), s32[]{:S(2)}) async-start(), calls=%async_computation.8 | async-start | bytes 9469952 | tf_op jit(solution)/shard_map/all_gather | solution.py:384
  27.8 6.7 copy-start.18
  27.8 6.8 copy-start.10
  27.8 7.7 copy-start.7
  27.8 122.6 %all-to-all-start = ((bf16[16,128,896]{1,2,0:T(8,128)(2,1)}), bf16[16,128,896]{1,2,0:T(8,128)(2,1)}, u32[]{:S(2)}, u32[]{:S(2)}) async-start(bf16[16,128,896]{1,2,0:T(8,128)(2,1)} %pad_maximum_fusion), calls=%async_computation | async-start | bytes 7340032 | tf_op jit(solution)/shard_map/all_to_all | solution.py:402
  34.3 428.7 %all-reduce.5.cloned.1.call-start = ((), (), s32[]{:S(2)}) async-start(), calls=%async_computation.7 | async-start | bytes 131072 | tf_op jit(solution)/shard_map/psum | solution.py:499
  166.5 2.3 copy-start.15
  221.7 6.2 copy-start
  240.3 3.2 copy-start.1
  256.0 4.1 copy-start.11
  256.6 1.9 copy-start.14
  264.4 11.0 %copy-start.5 = (bf16[16,128,896]{2,1,0:T(8,128)(2,1)S(1)}, bf16[16,128,896]{2,1,0:T(8,128)(2,1)}, u32[]{:S(2)}) copy-start(bf16[16,128,896]{2,1,0:T(8,128)(2,1)} %copy.137) | copy-start | bytes 11010052
  275.4 8.4 %copy-start.22 = (bf16[2048,512]{1,0:T(8,128)(2,1)}, bf16[2048,512]{1,0:T(8,128)(2,1)S(1)}, u32[]{:S(2)}) copy-start(bf16[2048,512]{1,0:T(8,128)(2,1)S(1)} %get-tuple-element.97) | copy-start | bytes 6291460
  275.4 8.4 %copy-start.13 = (bf16[16,128,128]{1,2,0:T(8,128)(2,1)S(1)}, bf16[16,128,128]{1,2,0:T(8,128)(2,1)}, u32[]{:S(2)}) copy-start(bf16[16,128,128]{1,2,0:T(8,128)(2,1)} %convolution_convert_fusion.4) | copy-start | bytes 1572868
  300.0 251.5 %reduce-scatter.5.cloned.1.call-start = ((), (), s32[]{:S(2)}) async-start(), calls=%async_computation.6 | async-start | bytes 8912896 | tf_op jit(solution)/shard_map/reduce_scatter | solution.py:469
  300.0 1.0 copy-start.12
  300.5 357.9 %reduce-scatter.3.cloned.1.call-start = ((), (), s32[]{:S(2)}) async-start(), calls=%async_computation.4 | async-start | bytes 8912896 | tf_op jit(solution)/shard_map/reduce_scatter | solution.py:436
  301.0 2.4 copy-start.4
  301.5 11.3 %copy-start.20 = (bf16[16,128,128]{1,2,0:T(8,128)(2,1)}, bf16[16,128,128]{1,2,0:T(8,128)(2,1)S(1)}, u32[]{:S(2)}) copy-start(bf16[16,128,128]{1,2,0:T(8,128)(2,1)S(1)} %convolution_convert_fusion.3) | copy-start | bytes 1572868
  348.2 8.1 copy-start.3
  348.2 8.1 copy-start.23
  363.4 5.4 copy-start.21
  363.4 85.4 %all-to-all-start.1 = ((bf16[16,128,896]{2,1,0:T(8,128)(2,1)}), bf16[16,128,896]{2,1,0:T(8,128)(2,1)}, u32[]{:S(2)}, u32[]{:S(2)}) async-start(bf16[16,128,896]{2,1,0:T(8,128)(2,1)} %pad_maximum_fusion.1), calls=%async_computation.3 | async-start | bytes 7340032 | tf_op jit(solution)/shard_map/all_to_all | solution.py:480
  368.7 445.2 %all-reduce.7.cloned.1.call-start = ((), (), s32[]{:S(2)}) async-start(), calls=%async_computation.9 | async-start | bytes 12582912 | tf_op jit(solution)/shard_map/psum | solution.py:506
  455.7 1.3 copy-start.2
  456.9 201.5 %copy-start.8 = (bf16[128,2048]{1,0:T(8,128)(2,1)S(1)}, bf16[128,2048]{1,0:T(8,128)(2,1)}, u32[]{:S(2)}) copy-start(bf16[128,2048]{1,0:T(8,128)(2,1)} %param.31) | copy-start | bytes 1572868
  456.9 201.5 %copy-start.17 = (f32[128]{0:T(128)S(1)}, f32[128]{0:T(128)}, u32[]{:S(2)}) copy-start(f32[128]{0:T(128)} %copy-done.16) | copy-start | bytes 1540
  464.3 361.8 %copy-start.19 = (f32[128]{0:T(128)}, f32[128]{0:T(128)S(1)}, u32[]{:S(2)}) copy-start(f32[128]{0:T(128)S(1)} %get-tuple-element.163) | copy-start | bytes 1540
  819.1 4.4 copy-start.6
Sparse Core Ops, SparseCore 0:
  10.7 127.0 all-gather.4
  140.7 80.8 all-gather.6
  300.1 142.8 all-reduce.4
  446.8 104.5 reduce-scatter.4
  555.4 103.0 reduce-scatter.2
  662.1 151.7 all-reduce.6

commit v2 on v1

--- a/solution.py
+++ b/solution.py
@@ -3,6 +3,8 @@
 import jax
 import jax.numpy as jnp
 from jax import lax
+from jax.experimental import pallas as pl
+from jax.experimental.pallas import tpu as pltpu
 from jax.sharding import PartitionSpec as P
 
 D = 2048
@@ -322,6 +324,423 @@
         summed[10],
         summed[11],
     )
+
+
+MESH = pl.DeviceIdType.MESH
+bf = jnp.bfloat16
+f32 = jnp.float32
+
+
+def gather_kernel(x_ref, bg_ref, sm_ref, jw_ref, ew_ref, X, BG, SM, WJ, WE,
+       tmp, su, sd, sy, ss, rx, bu, bd, by, bs, rb, sw, rw, sxw, rxw, lsem, ssm, rsm):
+    r = lax.axis_index("rep"); f = lax.axis_index("fsdp")
+    z = f // 4; y = (f // 2) % 2; c = f % 2
+    sib = z * 4 + y * 2 + (1 - c)
+    yp = z * 4 + (1 - y) * 2 + c
+    barrier = pltpu.get_barrier_semaphore()
+    @pl.loop(1, 16)
+    def _(k):
+        pl.semaphore_signal(barrier, inc=1, device_id=(r, (f + k) % 16), device_id_type=MESH)
+    pl.semaphore_signal(barrier, inc=1, device_id=(1 - r, f), device_id_type=MESH)
+    pl.semaphore_wait(barrier, 16)
+
+    def rc(src, dst, s, q, dev):
+        return pltpu.make_async_remote_copy(src_ref=src, dst_ref=dst, send_sem=s, recv_sem=q, device_id=dev, device_id_type=MESH)
+
+    def gather(own, OUT, su, sd, sy, ss, rr):
+        def item(i):
+            return OUT.at[i]
+        def up(i, src=None):
+            return rc(item(i) if src is None else src, item(i), su.at[i], rr.at[i], (r, f + 4))
+        def dn(i, src=None):
+            return rc(item(i) if src is None else src, item(i), sd.at[i], rr.at[i], (r, f - 4))
+        def ac(i, src=None):
+            return rc(item(i) if src is None else src, item(i), sy.at[i], rr.at[i], (r, yp))
+        def sb(i, src=None):
+            return rc(item(i) if src is None else src, item(i), ss.at[i], rr.at[i], (r, sib))
+        def begin():
+            pl.when(z < 3)(lambda: up(f, own).start())
+            pl.when(z > 0)(lambda: dn(f, own).start())
+            ac(f, own).start()
+            sb(f, own).start()
+        def step(s):
+            @pl.when(z - s >= 0)
+            def _():
+                i = f - 4 * s
+                up(i).wait_recv()
+                pl.when(z < 3)(lambda: up(i).start())
+                ac(i).start()
+                sb(i).start()
+            @pl.when(z + s <= 3)
+            def _():
+                i = f + 4 * s
+                dn(i).wait_recv()
+                pl.when(z > 0)(lambda: dn(i).start())
+                ac(i).start()
+                sb(i).start()
+        def ystep(s):
+            if s == 0:
+                ac(yp).wait_recv(); sb(yp).start()
+            else:
+                @pl.when(z - s >= 0)
+                def _():
+                    i = yp - 4 * s
+                    ac(i).wait_recv(); sb(i).start()
+                @pl.when(z + s <= 3)
+                def _():
+                    i = yp + 4 * s
+                    ac(i).wait_recv(); sb(i).start()
+        def finish():
+            @pl.loop(0, 8)
+            def _(k):
+                i = 2 * k + (1 - c)
+                sb(i).wait_recv()
+            @pl.loop(0, 8)
+            def _(k):
+                i = 2 * k + c
+                sb(i).wait_send()
+            @pl.loop(0, 4)
+            def _(k):
+                i = k * 4 + y * 2 + c
+                ac(i).wait_send()
+                pl.when((k <= z) & (z < 3))(lambda: up(i).wait_send())
+                pl.when((k >= z) & (z > 0))(lambda: dn(i).wait_send())
+        return begin, step, ystep, finish
+
+    xb, xs, xy, xf = gather(x_ref, X, su, sd, sy, ss, rx)
+    gb, gs, gy, gf = gather(bg_ref, BG, bu, bd, by, bs, rb)
+
+    def wpieces(src_dev, dst_dev, src_is_arg):
+        rows = pl.ds(pl.multiple_of(128 * src_dev + 64 * r, 64), 64)
+        out = []
+        for t in range(3):
+            if src_is_arg:
+                s = jw_ref.at[pl.ds(pl.multiple_of(64 * r, 64), 64), pl.ds(pl.multiple_of(2048 * t + 128 * dst_dev, 128), 128)]
+            else:
+                s = WJ.at[rows, pl.ds(128 * t, 128)]
+            out.append((s, WJ.at[rows, pl.ds(128 * t, 128)]))
+        if src_is_arg:
+            s = ew_ref.at[pl.ds(pl.multiple_of(64 * r, 64), 64), pl.ds(pl.multiple_of(512 * dst_dev, 512), 512)]
+        else:
+            s = WE.at[rows]
+        out.append((s, WE.at[rows]))
+        return out
+
+    a = pltpu.make_async_copy(x_ref, tmp.at[0], lsem.at[0]); a.start()
+    b = pltpu.make_async_copy(bg_ref, tmp.at[1], lsem.at[1]); b.start()
+    xb()
+    @pl.loop(1, 16)
+    def _(k):
+        fd = (f + k) % 16
+        rc(sm_ref, SM.at[f], ssm.at[fd], rsm.at[f], (r, fd)).start()
+        for t, (s, d) in enumerate(wpieces(f, fd, True)):
+            rc(s, d, sw.at[fd, t], rw.at[f, t], (r, fd)).start()
+    for t, (s, d) in enumerate(wpieces(f, f, True)):
+        rc(s, d, sxw.at[f, t], rxw.at[f, t], (1 - r, f)).start()
+        pltpu.make_async_copy(s, d, rw.at[f, t]).start()
+    own_small = pltpu.make_async_copy(sm_ref, SM.at[f], rsm.at[f])
+    own_small.start()
+    a.wait(); b.wait()
+    a2 = pltpu.make_async_copy(tmp.at[0], X.at[f], lsem.at[0]); a2.start()
+    b2 = pltpu.make_async_copy(tmp.at[1], BG.at[f], lsem.at[1]); b2.start()
+    def fwd(lo, hi):
+        @pl.loop(lo, hi)
+        def _(k):
+            fs = (f + 16 - k) % 16
+            for t, (s, d) in enumerate(wpieces(fs, f, False)):
+                rc(s, d, sw.at[fs, t], rw.at[fs, t], (r, f)).wait_recv()
+                rc(s, d, sxw.at[fs, t], rxw.at[fs, t], (1 - r, f)).start()
+    xs(1); xy(0); fwd(1, 5)
+    xs(2); xy(1); fwd(5, 9)
+    xs(3); xy(2); fwd(9, 13)
+    gb()
+    xy(3); fwd(13, 16)
+    for t, (s, d) in enumerate(wpieces(f, f, True)):
+        pltpu.make_async_copy(s, d, rw.at[f, t]).wait()
+    xf()
+    for s in (1, 2, 3):
+        gs(s)
+        gy(s - 1)
+    gy(3)
+    rows_of = lambda src: pl.ds(pl.multiple_of(128 * src + 64 * (1 - r), 64), 64)
+    @pl.loop(0, 16)
+    def _(fs):
+        for t in range(4):
+            d = WJ.at[rows_of(fs), pl.ds(128 * t, 128)] if t < 3 else WE.at[rows_of(fs)]
+            q = rc(d, d, sxw.at[fs, t], rxw.at[fs, t], (1 - r, f))
+            q.wait_recv()
+            q.wait_send()
+        @pl.when(fs != f)
+        def _():
+            for t, (s, d) in enumerate(wpieces(f, fs, True)):
+                rc(s, d, sw.at[fs, t], rw.at[f, t], (r, fs)).wait_send()
+    gf()
+    own_small.wait()
+    @pl.loop(1, 16)
+    def _(k):
+        fs = (f + k) % 16
+        other = rc(sm_ref, SM.at[fs], ssm.at[fs], rsm.at[fs], (r, fs))
+        other.wait_recv()
+        other.wait_send()
+    a2.wait(); b2.wait()
+
+def gather_all(x, bg, sm, jw, ew):
+    D = pltpu.SemaphoreType.DMA
+    hbm = pl.BlockSpec(memory_space=pl.ANY)
+    return pl.pallas_call(
+        gather_kernel,
+        out_shape=(jax.ShapeDtypeStruct((16, 128, 2048), bf), jax.ShapeDtypeStruct((16, 128, 2048), bf), jax.ShapeDtypeStruct((16, 16, 128), bf),
+                   jax.ShapeDtypeStruct((2048, 384), bf), jax.ShapeDtypeStruct((2048, 512), bf)),
+        in_specs=[hbm] * 5, out_specs=(hbm,) * 5,
+        scratch_shapes=[pltpu.VMEM((2, 128, 2048), bf)] + [D((16,))] * 10 + [D((16, 4))] * 4 + [D((2,)), D((16,)), D((16,))],
+        compiler_params=pltpu.CompilerParams(collective_id=0, has_side_effects=True, vmem_limit_bytes=60 << 20),
+    )(x, bg, sm, jw, ew)
+
+
+def reduce_kernel(P1, P2, OS, JE, SO1, SO2, OSo, JW, EW, L, A, B, CO, CI, HB, RX, LOS, ROS,
+       sl, sa, ra, sb, rb, sc, rco, rci, sx, rx, so, ro, so2, ro2, sw, rw, sf, rf, lsem):
+    r = lax.axis_index("rep"); f = lax.axis_index("fsdp")
+    z = f // 4; y = (f // 2) % 2; c = f % 2
+    sib = (r, z * 4 + y * 2 + (1 - c))
+    yp = (r, z * 4 + (1 - y) * 2 + c)
+    xp = (1 - r, f)
+    lower = z <= 1
+    zz = jnp.where(lower, z, 3 - z)
+    def phys(q):
+        return jnp.where(lower, q, 3 - q)
+    f_in = (r, jnp.where(lower, f + 4, f - 4))
+    f_out = (r, jnp.where(lower, f - 4, f + 4))
+    barrier = pltpu.get_barrier_semaphore()
+    @pl.loop(1, 16)
+    def _(k):
+        pl.semaphore_signal(barrier, inc=1, device_id=(r, (f + k) % 16), device_id_type=MESH)
+    pl.semaphore_signal(barrier, inc=1, device_id=xp, device_id_type=MESH)
+    pl.semaphore_wait(barrier, 16)
+
+    def rc(src, dst, s, q, dev):
+        return pltpu.make_async_remote_copy(src_ref=src, dst_ref=dst, send_sem=s, recv_sem=q, device_id=dev, device_id_type=MESH)
+    def lc(src, dst, s):
+        return pltpu.make_async_copy(src, dst, s)
+
+    def add_into(dst, src, rows):
+        @pl.loop(0, rows // 16)
+        def _(i):
+            w = pl.ds(pl.multiple_of(i * 16, 16), 16)
+            dst[w] = (dst[w].astype(f32) + src[w].astype(f32)).astype(bf)
+
+    def reducer(n, PP, SO):
+        def a_send(k):
+            return rc(PP.at[2 * k + 1 - c], A.at[n, k], sa.at[n, k], ra.at[n, k], sib)
+        def a_load(k):
+            return lc(PP.at[2 * k + c], L.at[n, k], sl.at[n, k])
+        def b_send(zp):
+            return rc(L.at[n, zp * 2 + 1 - y], B.at[n, zp], sb.at[n, zp], rb.at[n, zp], yp)
+        def order():
+            return (3, 0, 2, 1)
+        def begin():
+            for yy in (1 - y, y):
+                for q in order():
+                    k = phys(q) * 2 + yy
+                    a_send(k).start()
+                    a_load(k).start()
+        def prep(k):
+            a_load(k).wait()
+            a_send(k).wait_recv()
+            add_into(L.at[n, k], A.at[n, k], 128)
+        def far():
+            for q in order():
+                prep(phys(q) * 2 + 1 - y)
+                b_send(phys(q)).start()
+        def near(q):
+            zp = phys(q)
+            k = zp * 2 + y
+            prep(k)
+            b_send(zp).wait_recv()
+            add_into(L.at[n, k], B.at[n, zp], 128)
+        def to_in(q):
+            zp = phys(q)
+            return zp, L.at[n, zp * 2 + y]
+        def recv(buf, q, sem):
+            zp = phys(q)
+            rc(buf.at[n, zp], buf.at[n, zp], sc.at[n, zp], sem.at[n, zp], f_in).wait_recv()
+            return buf.at[n, zp]
+        def send(q, buf, sem, dev):
+            zp = phys(q)
+            return rc(L.at[n, zp * 2 + y], buf.at[n, zp], sc.at[n, zp], sem.at[n, zp], dev)
+        def step(q):
+            near(q)
+            zp = phys(q)
+            k = zp * 2 + y
+            @pl.when(zz == 0)
+            def _():
+                if q > 0:
+                    send(q, CO, rco, f_in).start()
+            @pl.when(zz == 1)
+            def _():
+                if q >= 2:
+                    add_into(L.at[n, k], recv(CO, q, rco), 128)
+                    send(q, CI, rci, f_in).start()
+                if q == 0:
+                    add_into(L.at[n, k], recv(CI, q, rci), 128)
+                    send(q, CI, rci, f_out).start()
+        def last():
+            def total(q, bufs):
+                k = phys(q) * 2 + y
+                @pl.loop(0, 8)
+                def _(i):
+                    w = pl.ds(pl.multiple_of(i * 16, 16), 16)
+                    v = L[n, k, w].astype(f32)
+                    for b in bufs:
+                        v = v + b[w].astype(f32)
+                    SO[w] = v
+            @pl.when(zz == 0)
+            def _():
+                total(0, [recv(CI, 0, rci)])
+            @pl.when(zz == 1)
+            def _():
+                total(1, [recv(CO, 1, rco), recv(CI, 1, rci)])
+        def drain():
+            @pl.loop(0, 8)
+            def _(k):
+                a_send(k).wait_send()
+            @pl.loop(0, 4)
+            def _(zp):
+                b_send(zp).wait_send()
+            for q in range(4):
+                if q > 0:
+                    pl.when(zz == 0)(lambda: send(q, CO, rco, f_in).wait_send())
+                if q != 1:
+                    pl.when(zz == 1)(lambda: send(q, CI, rci, f_in).wait_send())
+        return begin, far, step, last, drain
+
+    R1 = reducer(0, P1, SO1)
+    R2 = reducer(1, P2, SO2)
+
+    def x1(g):
+        return rc(JE.at[pl.ds(4 * g, 4), 1 - r], RX.at[pl.ds(4 * g, 4)], sx.at[g], rx.at[g], xp)
+    def hb_load():
+        return lc(JE.at[:, r], HB, lsem.at[0])
+    rr = pl.ds(pl.multiple_of(64 * r, 64), 64)
+    def dst(fs, t):
+        if t < 3:
+            return JW.at[rr, pl.ds(pl.multiple_of(2048 * t + 128 * fs, 128), 128)]
+        return EW.at[rr, pl.ds(pl.multiple_of(512 * fs, 512), 512)]
+    def srcp(fd, t):
+        return HB.at[fd, :, pl.ds(128 * t, 128)] if t < 3 else HB.at[fd, :, pl.ds(384, 512)]
+    def dsto(fs, t):
+        ro_ = pl.ds(pl.multiple_of(64 * (1 - r), 64), 64)
+        if t < 3:
+            return JW.at[ro_, pl.ds(pl.multiple_of(2048 * t + 128 * fs, 128), 128)]
+        return EW.at[ro_, pl.ds(pl.multiple_of(512 * fs, 512), 512)]
+    def je_group(g):
+        if g == 0: hb_load().wait()
+        x1(g).wait_recv()
+        @pl.loop(0, 4)
+        def _(j):
+            fd = 4 * g + j
+            add_into(HB.at[fd], RX.at[fd], 64)
+            @pl.when(fd != f)
+            def _():
+                for t in range(4):
+                    rc(srcp(fd, t), dst(f, t), sw.at[fd, t], rw.at[f, t], (r, fd)).start()
+            @pl.when(fd == f)
+            def _():
+                for t in range(4):
+                    lc(srcp(fd, t), dst(f, t), sw.at[fd, t]).start()
+                    rc(srcp(fd, t), dst(f, t), sf.at[fd, t], rf.at[f, t], xp).start()
+    def fwd_group(g):
+        @pl.loop(4 * g, 4 * g + 4)
+        def _(fs):
+            @pl.when(fs != f)
+            def _():
+                for t in range(4):
+                    rc(dst(fs, t), dst(fs, t), sw.at[fs, t], rw.at[fs, t], xp).wait_recv()
+                    rc(dst(fs, t), dst(fs, t), sf.at[fs, t], rf.at[fs, t], xp).start()
+    def je_drain():
+        for g in range(4):
+            x1(g).wait_send()
+        @pl.loop(0, 16)
+        def _(fs):
+            for t in range(4):
+                rc(dsto(fs, t), dsto(fs, t), sf.at[fs, t], rf.at[fs, t], xp).wait_recv()
+                rc(dsto(fs, t), dsto(fs, t), sf.at[fs, t], rf.at[fs, t], xp).wait_send()
+            @pl.when(fs != f)
+            def _():
+                for t in range(4):
+                    rc(srcp(fs, t), dst(f, t), sw.at[fs, t], rw.at[f, t], xp).wait_send()
+            @pl.when(fs == f)
+            def _():
+                for t in range(4):
+                    lc(srcp(fs, t), dst(f, t), sw.at[fs, t]).wait()
+
+    def o1(j):
+        return rc(OS.at[1 - r, j], ROS.at[j], so.at[j], ro.at[j], xp)
+    def o2(j):
+        return rc(LOS.at[j], OSo.at[r, j], so2.at[j], ro2.at[j], xp)
+    def o2r(j):
+        return rc(LOS.at[j], OSo.at[1 - r, j], so2.at[j], ro2.at[j], xp)
+    def os_load():
+        return lc(OS.at[r], LOS, lsem.at[1])
+    def os_store(j):
+        return lc(LOS.at[j], OSo.at[r, j], lsem.at[2 + j])
+    def os_step(j):
+        if j == 0: os_load().wait()
+        o1(j).wait_recv()
+        add_into(LOS.at[j], ROS.at[j], 64)
+        o2(j).start()
+        os_store(j).start()
+    def os_drain():
+        for j in range(5):
+            o1(j).wait_send(); o2(j).wait_send(); o2r(j).wait_recv(); os_store(j).wait()
+
+    hb_load().start()
+    for g in range(4): x1(g).start()
+    os_load().start()
+    for j in range(5): o1(j).start()
+    R1[0]()
+    R1[1]()
+    R2[0]()
+    R1[2](3)
+    je_group(0)
+    R1[2](0)
+    je_group(1)
+    R1[2](2); R2[1]()
+    je_group(2)
+    R1[2](1)
+    je_group(3)
+    os_step(0); os_step(1)
+    R1[3](); R2[2](3)
+    os_step(2); os_step(3); os_step(4)
+    fwd_group(0)
+    R2[2](0)
+    fwd_group(1)
+    R2[2](2)
+    fwd_group(2)
+    R2[2](1)
+    fwd_group(3)
+    R2[3]()
+    je_drain(); os_drain()
+    R1[4](); R2[4]()
+
+def reduce_all(p1, p2, os_, je):
+    D = pltpu.SemaphoreType.DMA
+    hbm = pl.BlockSpec(memory_space=pl.ANY)
+    vm = pl.BlockSpec(memory_space=pltpu.VMEM)
+    S = jax.ShapeDtypeStruct
+    return pl.pallas_call(
+        reduce_kernel,
+        out_shape=(S((128, 2048), f32), S((128, 2048), f32), S((2, 5, 64, 2048), bf), S((128, 6144), bf), S((128, 8192), bf)),
+        in_specs=[hbm] * 4, out_specs=(vm, vm, hbm, hbm, hbm),
+        scratch_shapes=[
+            pltpu.VMEM((2, 8, 128, 2048), bf), pltpu.VMEM((2, 8, 128, 2048), bf), pltpu.VMEM((2, 4, 128, 2048), bf),
+            pltpu.VMEM((2, 4, 128, 2048), bf), pltpu.VMEM((2, 4, 128, 2048), bf),
+            pltpu.VMEM((16, 64, 896), bf), pltpu.VMEM((16, 64, 896), bf),
+            pltpu.VMEM((5, 64, 2048), bf), pltpu.VMEM((5, 64, 2048), bf),
+            D((2, 8)), D((2, 8)), D((2, 8)), D((2, 4)), D((2, 4)), D((2, 4)), D((2, 4)), D((2, 4)),
+            D((4,)), D((4,)), D((5,)), D((5,)), D((5,)), D((5,)),
+            D((16, 4)), D((16, 4)), D((16, 4)), D((16, 4)), D((8,))],
+        compiler_params=pltpu.CompilerParams(collective_id=1, has_side_effects=True, vmem_limit_bytes=60 << 20),
+    )(p1, p2, os_, je)
 
 
 def wide(a):
@@ -379,12 +798,13 @@
             segment[0].astype(low),
         ]
     )
-    small = jnp.pad(small, (0, -small.shape[0] % width)).reshape(-1, width)
-    extra = small.shape[0]
-    rows_all = lax.all_gather(jnp.concatenate([layer_input, small], 0), "fsdp", axis=0)
-    small_all = rows_all[:, own:].reshape(n, extra * width)
-    rows = wide(rows_all[:, :own]).reshape(tokens, width)
-    branch = lax.all_gather(branch_own, "fsdp", axis=0, tiled=True)
+    small = jnp.pad(small, (0, 2048 - small.shape[0])).reshape(16, 128)
+    rows_all, branch_all, small_all, weight_j, weight_e = gather_all(
+        layer_input, branch_own, small, joined_weight, expand_weight
+    )
+    small_all = small_all.reshape(n, 2048)
+    rows = wide(rows_all).reshape(tokens, width)
+    branch = branch_all.reshape(tokens, width)
     gain_one, shift_one, gain_two, shift_two, bias_o, bias_s = (
         wide(small_all[:, k * part : (k + 1) * part]).reshape(width) for k in range(6)
     )
@@ -392,15 +812,6 @@
     bias_j = lax.dynamic_index_in_dim(bias_j, me, 1, keepdims=False).reshape(3 * cols)
     seg_all = small_all[:, 6 * part + third : 6 * part + third + own]
 
-    sent = jnp.concatenate(
-        [
-            joined_weight.reshape(part, 3, n, cols).transpose(2, 0, 1, 3).reshape(n, part, 3 * cols),
-            expand_weight.reshape(part, n, piece).transpose(1, 0, 2),
-        ],
-        2,
-    )
-    held = lax.all_to_all(sent, "fsdp", 0, 0).reshape(width, 3 * cols + piece)
-    weight_j, weight_e = (held[:, : 3 * cols], held[:, 3 * cols :])
     weight_os = jnp.concatenate([output_weight, shrink_weight], 0)
 
     normalized, inverse = normalize(rows)
@@ -433,10 +844,6 @@
     slope = gelu_slope(expanded)
     inner = jnp.concatenate([mixed, activated], 1)
     partial = jnp.dot(inner, weight_os, preferred_element_type=jnp.float32).astype(low)
-    summed = lax.psum_scatter(partial, "fsdp", scatter_dimension=0, tiled=True)
-    layer_output = (
-        wide(layer_input) + live_rows * (wide(summed) + (bias_o + bias_s))
-    ).astype(low)
 
     grad_os = jnp.einsum("tf,td->fd", inner, branch, preferred_element_type=jnp.float32)
     inner_grad = jnp.einsum("td,fd->tf", branch, weight_os, preferred_element_type=jnp.float32)
@@ -466,7 +873,18 @@
     back_one = jnp.einsum("te,de->td", joined_grad, weight_j, preferred_element_type=jnp.float32)
     back_two = jnp.einsum("tf,df->td", expanded_grad, weight_e, preferred_element_type=jnp.float32)
     hat = (back_one * gain_one + back_two * gain_two).astype(low)
-    hat_own = wide(lax.psum_scatter(hat, "fsdp", scatter_dimension=0, tiled=True))
+    grads = jnp.concatenate([grad_j, grad_e], 1).astype(low)
+    summed, hat_own, rest_os, joined_weight_grad, expand_weight_grad = reduce_all(
+        partial.reshape(n, own, width),
+        hat.reshape(n, own, width),
+        grad_os.astype(low).reshape(2, 5, 64, width),
+        grads.reshape(n, 2, part // 2, 3 * cols + piece),
+    )
+    rest_os = wide(rest_os).reshape(cols + piece, width)
+    layer_output = (
+        wide(layer_input) + live_rows * (summed + (bias_o + bias_s))
+    ).astype(low)
+
     rows_own = wide(layer_input)
     normalized_own, inverse_own = normalize(rows_own)
     row_grad = inverse_own * (
@@ -475,13 +893,6 @@
         - normalized_own * jnp.mean(hat_own * normalized_own, -1, keepdims=True)
     )
     input_grad = (seeds + row_grad).astype(low)
-
-    grads = jnp.concatenate([grad_j, grad_e], 1).astype(low).reshape(n, part, 3 * cols + piece)
-    grads = lax.all_to_all(grads, "fsdp", 0, 0)
-    joined_weight_grad = (
-        grads[:, :, : 3 * cols].reshape(n, part, 3, cols).transpose(1, 2, 0, 3).reshape(part, 3 * width)
-    )
-    expand_weight_grad = grads[:, :, 3 * cols :].transpose(1, 0, 2).reshape(part, n * piece)
 
     vectors = jnp.stack(
         [
@@ -503,38 +914,28 @@
     pieces = lax.dynamic_index_in_dim(pieces, me, 1, keepdims=False)
     joined_bias_grad = lax.dynamic_slice(small_sums, (5 * width + me * third,), (third,))
     expand_bias_grad = jnp.sum(wide(expanded_grad), 0)
-    rest = lax.psum(
-        (
-            joined_weight_grad,
-            expand_weight_grad,
-            grad_os[:cols].astype(low),
-            grad_os[cols:].astype(low),
-            expand_bias_grad.astype(low),
-        ),
-        "rep",
-    )
-    rest = tuple(wide(a) for a in rest)
+    expand_bias_grad = wide(lax.psum(expand_bias_grad.astype(low), "rep"))
     return (
         layer_output,
         input_grad,
         pieces[0],
         pieces[1],
-        rest[0],
+        wide(joined_weight_grad),
         joined_bias_grad,
-        rest[2],
+        rest_os[:cols],
         pieces[4],
         pieces[2],
         pieces[3],
-        rest[1],
-        rest[4],
-        rest[3],
+        wide(expand_weight_grad),
+        expand_bias_grad,
+        rest_os[cols:],
         pieces[4],
     )
 
 
 def solution(mesh):
     n = mesh.shape["fsdp"]
-    chosen = functools.partial(head_body, n) if HEADS % n == 0 else body
+    chosen = functools.partial(head_body, n) if n == HEADS else body
     placed = (
         P(("rep", "fsdp"), None),
         P(("rep", "fsdp"), None),

time: 841 us -> 532 us (0.63)
  waiting for transfers between devices: 580 us -> 0.02 us
  Pallas kernels: 0 us -> 310 us
  local copies, waits for them, and re-layouts: 81.3 us -> 53.8 us
  starting transfers between devices: 12.2 us -> 0.04 us
  other arithmetic: 52.2 us -> 42 us
  matrix products: 88.4 us -> 98.1 us
    pallas_call x0 -> x2, Pallas kernels: none -> 310 us  [the longest x1 175 us: reduce_all(): pl.pallas_call(reduce_kernel, out_shape=(S((128, 2048), f32), S((128, 204...]
    reduce_scatter x2 -> x0, waiting for transfers between devices: 191 us -> none  [the longest x1 106 us: head_body(): summed = lax.psum_scatter(partial, 'fsdp', scatter_dimension=0, tiled=True)]
    all_to_all x2 -> x0, waiting for transfers between devices: 183 us -> none  [the longest x1 113 us: head_body(): held = lax.all_to_all(sent, 'fsdp', 0, 0).reshape(width, 3 * cols + piece)]
    psum x1 -> x0, waiting for transfers between devices: 153 us -> none  [head_body(): lax.psum((joined_weight_grad, expand_weight_grad, grad_os[:cols].astype(l...]
    all_gather x2 -> x0, waiting for transfers between devices: 52 us -> none  [the longest x1 52 us: head_body(): lax.all_gather(jnp.concatenate([layer_input, small], 0), 'fsdp', axis=0)]
    all_to_all x2 -> x0, starting transfers between devices: 11.8 us -> none  [the longest x1 6.5 us: head_body(): held = lax.all_to_all(sent, 'fsdp', 0, 0).reshape(width, 3 * cols + piece)]
    unnamed x65 -> x71, local copies, waits for them, and re-layouts: 28.1 us -> 16.8 us
    convert_element_type x1 -> x0, other arithmetic: 9.41 us -> none  [head_body(): activated = jax.nn.gelu(expanded, approximate=False).astype(low)]
  transfers between devices with their start and end apart: 8 -> 1, of which waited for: 6 -> 0; matrix products, arithmetic and copies ran while one was open for 15% -> 15% of each run, Pallas kernels for 0% -> 33%
where the time goes in v2:
time: 532 us; the launch traced here: 524 us
  Pallas kernels  310 us (58%)
  matrix products  98.1 us (18%)
  local copies, waits for them, and re-layouts  53.8 us (10%)
  other arithmetic  42 us (8%)
  between operations  14.9 us (3%)
    pallas_call x1, Pallas kernels, reduce_all(): pl.pallas_call(reduce_kernel, out_shape=(S((128, 2048), f32), S((128, 204...  175 us
    pallas_call x1, Pallas kernels, gather_all(): pl.pallas_call(gather_kernel, out_shape=(jax.ShapeDtypeStruct((16, 128, 2...  134 us
    dot_general x1, matrix products, head_body(): jnp.dot(normed_two, weight_e, preferred_element_type=jnp.float32)  17 us
    unnamed x71, local copies, waits for them, and re-layouts  16.8 us
    dot_general x1, matrix products, head_body(): jnp.einsum('te,de->td', joined_grad, weight_j, preferred_element_type=jnp...  14.9 us
    dot_general x1, local copies, waits for them, and re-layouts, head_body(): jnp.einsum('td,tf->df', normed_two, expanded_grad, preferred_element_type...  12.7 us
    dot_general x1, local copies, waits for them, and re-layouts, head_body(): jnp.einsum('td,te->de', normed_one, joined_grad, preferred_element_type=j...  12.4 us
  transfers between devices with their start and end apart: 1, of which 0 were waited for; matrix products, arithmetic and copies ran while one was open for 15% of the time, Pallas kernels for 33%

profile of v2, /device:TPU:10, one launch (start us, length us, event | category | flops | bytes accessed | tf_op | source)
XLA Modules:
  0.0 523.5 jit_solution(583403286071637116)
XLA Ops:
  7.3 0.7 convert_bitcast_fusion.1
  7.9 0.7 convert_bitcast_fusion
  8.6 0.8 dynamic-update-slice.2
  9.4 0.8 dynamic-update-slice.3
  10.3 0.8 dynamic-update-slice.4
  11.1 0.8 dynamic-update-slice.5
  11.9 0.8 dynamic-update-slice.6
  12.8 0.8 dynamic-update-slice.7
  13.6 0.9 dynamic-update-slice.8
  14.7 0.6 pad_bitcast_fusion.sm_ref
  15.2 2.0 convert_reduce_fusion.3
  17.3 134.2 %shard_map.263 = (bf16[16,128,2048]{2,1,0:T(8,128)(2,1)}, bf16[16,128,2048]{2,1,0:T(8,128)(2,1)}, bf16[16,16,128]{2,1,0:T(8,128)(2,1)}, bf16[2048,384]{1,0:T(8,128)(2,1)}, bf16[2048,512]{1,0:T(8,128)(2,1)}) custom-call(bf16[128,2048]{1,0:T(8,128)(2,1)} %x_ref.1, bf16[128,2048]{1,0:T(8,128)(2,1)} %get-tuple-element.45.bg_ref, ...), custom_call_target="tpu_custom_call" | custom-call | tf_op jit(solution)/shard_map/pallas_call | solution.py:490
  151.5 0.9 copy.105
  152.4 4.7 convert_reduce_fusion
  157.1 1.0 copy-done
  158.2 2.4 multiply_reduce_fusion.2
  160.6 10.2 %add_convert_fusion.2 = (bf16[2048,2048]{1,0:T(8,128)(2,1)S(1)}, bf16[2048,2048]{1,0:T(8,128)(2,1)}) fusion(bf16[16,128,2048]{2,1,0:T(8,128)(2,1)} %get-tuple-element.24, f32[2048]{0:T(1024)S(1)} %get-tuple-element.64, f32[2048]{0:T(1024)S(1)} %get-tuple-element.65, f32[2048]{0:T(1024)S(1)} %rsqrt_bitcast_fusion, f32[2048]{0:T(1024)S(1)} %get-tuple-element.73, ...), kind=kLoop, calls=%fused_computation.7 | loop fusion | flops 37748736 | bytes 25214976 | tf_op jit(solution)/shard_map/convert_element_type | solution.py:818
  170.8 3.2 copy-done.1
  174.0 6.2 %convolution_add_fusion = f32[2048,384]{1,0:T(8,128)} fusion(bf16[2048,2048]{1,0:T(8,128)(2,1)S(1)} %get-tuple-element.47, bf16[2048,384]{1,0:T(8,128)(2,1)S(1)} %copy-done.24, f32[384]{0:T(512)S(1)} %bitcast.219), kind=kOutput, calls=%fused_computation.40 | convolution fusion | flops 3222011904 | bytes 13108736 | tf_op jit(solution)/shard_map/dot_general | solution.py:820
  180.2 2.4 copy.71
  182.6 0.7 copy.100
  183.5 0.8 copy-done.13
  184.4 0.6 convert_reduce_fusion.4
  185.3 10.2 %fusion.115 = f32[2048,640]{1,0:T(8,128)S(1)} fusion(bf16[2048,2048]{1,0:T(8,128)(2,1)} %bitcast.220, bf16[640,2048]{1,0:T(8,128)(2,1)S(1)} %constant_dynamic-update-slice_fusion), kind=kOutput, calls=%fused_computation.197 | convolution fusion | flops 5368709120 | bytes 16252928 | tf_op jit(solution)/shard_map/td,fd->tf/dot_general | solution.py:849
  195.6 2.3 copy-done.3
  197.9 0.8 slice.241
  198.7 0.5 copy.98
  199.2 0.6 copy_bitcast_fusion
  200.0 0.6 fusion.87
  200.6 1.1 fusion.114
  201.7 2.2 convolution_convert_fusion.4
  203.9 2.0 multiply_reduce_fusion.3
  205.9 0.7 multiply_convert_fusion
  207.0 0.5 fusion.27
  207.4 0.6 fusion.69
  208.1 0.6 fusion.75
  209.5 17.0 %fusion.4 = (bf16[2048,512]{1,0:T(8,128)(2,1)}, f32[2048,512]{1,0:T(8,128)S(1)}) fusion(f32[512]{0:T(512)S(1)} %convert_element_type.164, bf16[2048,2048]{1,0:T(8,128)(2,1)} %get-tuple-element.48, bf16[2048,512]{1,0:T(8,128)(2,1)} %get-tuple-element.27), kind=kOutput, calls=%fused_computation.15 | convolution fusion | flops 4364173312 | bytes 16779264 | tf_op jit(solution)/shard_map/dot_general | solution.py:842
  226.5 2.1 fusion.110
  228.6 8.4 %fusion.116 = f32[2048,2048]{1,0:T(8,128)} fusion(bf16[2048,512]{1,0:T(8,128)(2,1)S(1)} %get-tuple-element.43, bf16[2048,512]{1,0:T(8,128)(2,1)S(1)} %copy-done.23), kind=kOutput, calls=%fused_computation.198 | convolution fusion | flops 4294967296 | bytes 20971520 | tf_op jit(solution)/shard_map/tf,df->td/dot_general | solution.py:874
  237.5 14.9 %multiply_reduce_fusion.1 = (f32[2048]{0:T(1024)S(1)}, f32[2048]{0:T(1024)S(1)}, f32[2048]{0:T(1024)S(1)}, f32[2048]{0:T(1024)S(1)}, bf16[2048,2048]{1,0:T(8,128)(2,1)}) fusion(bf16[16,128,2048]{2,1,0:T(8,128)(2,1)} %get-tuple-element.24, f32[2048]{0:T(1024)S(1)} %rsqrt_bitcast_fusion, f32[2048]{0:T(1024)S(1)} %get-tuple-element.73, ...), kind=kOutput, calls=%fused_computation.4 | convolution fusion | flops 3280461824 | bytes 36765696 | tf_op jit(solution)/shard_map/te,de->td/dot_general | solution.py:873
  252.6 0.6 pad_maximum_fusion.17
  253.4 0.5 convolution_convert_fusion.3
  253.9 0.9 copy-done.26
  254.8 9.2 %convolution_convert_fusion.1 = bf16[640,2048]{1,0:T(8,128)(2,1)} fusion(bf16[2048,2048]{1,0:T(8,128)(2,1)} %bitcast.221, bf16[2048,512]{1,0:T(8,128)(2,1)S(1)} %copy-done.26, bf16[2048,128]{1,0:T(8,128)(2,1)S(1)} %bitcast.222), kind=kOutput, calls=%fused_computation.38 | convolution fusion | flops 5375262720 | bytes 13631488 | tf_op jit(solution)/shard_map/tf,td->fd/dot_general | solution.py:848
  264.1 8.9 %convolution_convert_fusion = bf16[2048,2048]{1,0:T(8,128)(2,1)} fusion(bf16[640,2048]{1,0:T(8,128)(2,1)S(1)} %copy-done.18, bf16[2048,512]{1,0:T(8,128)(2,1)S(1)} %copy-done.26, bf16[2048,128]{1,0:T(8,128)(2,1)S(1)} %bitcast.223), kind=kOutput, calls=%fused_computation.10 | convolution fusion | flops 5378146304 | bytes 13631488 | tf_op jit(solution)/shard_map/dot_general | solution.py:846
  273.2 12.7 %copy.88 = bf16[2048,2048]{1,0:T(8,128)(2,1)} copy(bf16[2048,2048]{0,1:T(8,128)(2,1)} %bitcast.185) | data formatting | bytes 16777216 | tf_op jit(solution)/shard_map/td,tf->df/dot_general | solution.py:872
  286.0 8.5 %fusion.20 = bf16[16,2,64,512]{3,2,1,0:T(8,128)(2,1)S(1)} fusion(bf16[16,2,64,2048]{3,2,1,0:T(8,128)(2,1)} %bitcast.190, bf16[2048,512]{1,0:T(8,128)(2,1)} %copy-done.8), kind=kOutput, calls=%fused_computation.45 | convolution fusion | flops 4296015872 | bytes 12582912 | tf_op jit(solution)/shard_map/td,tf->df/dot_general | solution.py:872
  294.5 12.4 %copy.87 = bf16[2048,2048]{1,0:T(8,128)(2,1)} copy(bf16[2048,2048]{0,1:T(8,128)(2,1)} %bitcast.184) | data formatting | bytes 16777216 | tf_op jit(solution)/shard_map/td,te->de/dot_general | solution.py:871
  306.9 8.1 %convolution_convert_fusion.2 = bf16[16,2,64,384]{3,2,1,0:T(8,128)(2,1)S(1)} fusion(bf16[16,2,64,2048]{3,2,1,0:T(8,128)(2,1)} %bitcast.189, bf16[2048,128]{1,0:T(8,128)(2,1)} %bitcast.204, bf16[2048,128]{1,0:T(8,128)(2,1)} %bitcast.201, bf16[2048,128]{1,0:T(8,128)(2,1)S(1)} %bitcast.198), kind=kOutput, calls=%fused_computation.46 | convolution fusion | flops 3226730496 | bytes 11534336 | tf_op jit(solution)/shard_map/td,te->de/dot_general | solution.py:871
  315.0 2.4 pad_maximum_fusion.JE
  317.5 175.3 %shard_map.264 = (f32[128,2048]{1,0:T(8,128)}, f32[128,2048]{1,0:T(8,128)}, bf16[2,5,64,2048]{3,2,1,0:T(8,128)(2,1)}, bf16[128,6144]{1,0:T(8,128)(2,1)}, bf16[128,8192]{1,0:T(8,128)(2,1)}) custom-call(bf16[16,128,2048]{2,1,0:T(8,128)(2,1)} %bitcast.192, bf16[16,128,2048]{2,1,0:T(8,128)(2,1)} %bitcast.191, bf16[2,5,64,2048]{3,2,1,0:T(8,128)(2,1)} %bitcast.195, ...), custom_call_target="tpu_custom_call" | custom-call | tf_op jit(solution)/shard_map/pallas_call | solution.py:730
  492.8 1.5 fusion.109
  494.4 2.6 bitcast_convert_fusion
  497.0 1.5 fusion.38
  498.5 1.0 slice.181
  499.6 2.3 slice.182
  501.8 5.0 psum.15
  506.9 0.6 convert_element_type.179
  507.5 3.4 convert_element_type.177
  510.9 2.4 convert_element_type.178
  513.3 0.8 slice.180
  514.1 0.5 fusion.92
  514.6 1.3 dynamic_slice.13
  516.0 0.5 copy.117
  (94 shorter events, 3.1 us)
Async XLA Ops:
  7.2 506.1 %all-reduce.3.cloned.1.call-start = ((), (), s32[]{:S(2)}) async-start(), calls=%async_computation | async-start | bytes 131072 | tf_op jit(solution)/shard_map/psum | solution.py:910
  7.9 149.2 %copy-start.19 = (f32[128]{0:T(128)}, f32[128]{0:T(128)S(1)}, u32[]{:S(2)}) copy-start(f32[128]{0:T(128)S(1)} %convert_bitcast_fusion.1) | copy-start | bytes 1540
  152.4 5.8 %copy-start = (bf16[16,128,2048]{2,1,0:T(8,128)(2,1)S(1)}, bf16[16,128,2048]{2,1,0:T(8,128)(2,1)}, u32[]{:S(2)}) copy-start(bf16[16,128,2048]{2,1,0:T(8,128)(2,1)} %get-tuple-element.24) | copy-start | bytes 25165828
  160.6 13.5 %copy-start.24 = (bf16[2048,384]{1,0:T(8,128)(2,1)S(1)}, bf16[2048,384]{1,0:T(8,128)(2,1)}, u32[]{:S(2)}) copy-start(bf16[2048,384]{1,0:T(8,128)(2,1)} %get-tuple-element.26) | copy-start | bytes 4718596
  170.8 3.2 copy-start.1
  183.3 1.0 copy-start.13
  183.3 1.8 copy-start.6
  185.3 10.3 %copy-start.17 = (bf16[640,2048]{1,0:T(8,128)(2,1)}, bf16[640,2048]{1,0:T(8,128)(2,1)S(1)}, u32[]{:S(2)}) copy-start(bf16[640,2048]{1,0:T(8,128)(2,1)S(1)} %constant_dynamic-update-slice_fusion) | copy-start | bytes 7864324
  195.6 2.3 copy-start.3
  199.2 4.7 copy-start.14
  201.7 4.2 copy-start.10
  203.9 33.1 %copy-start.16 = (bf16[16,128,128]{1,2,0:T(8,128)(2,1)}, bf16[16,128,128]{1,2,0:T(8,128)(2,1)S(1)}, u32[]{:S(2)}) copy-start(bf16[16,128,128]{1,2,0:T(8,128)(2,1)S(1)} %convolution_convert_fusion.4) | copy-start | bytes 1572868
  205.9 2.8 copy-start.21
  209.1 17.4 %slice-start = ((s8[5242880]{0:T(1024)(128)(4,1)}), s8[1048576]{0:T(1024)(128)(4,1)S(1)}, s32[]{:S(2)}) async-start(s8[5242880]{0:T(1024)(128)(4,1)} %bitcast.193), calls=%async_computation.1 | async-start | bytes 2097152
  209.4 28.0 %copy-start.7 = (bf16[16,128,1,128]{3,1,0,2:T(8,128)(2,1)}, bf16[16,128,1,128]{3,1,0,2:T(8,128)(2,1)S(1)}, u32[]{:S(2)}) copy-start(bf16[16,128,1,128]{3,1,0,2:T(8,128)(2,1)S(1)} %copy.85) | copy-start | bytes 1572868
  209.4 17.0 %slice-start.1 = ((s8[5242880]{0:T(1024)(128)(4,1)}), s8[4194304]{0:T(1024)(128)(4,1)S(1)}, s32[]{:S(2)}) async-start(s8[5242880]{0:T(1024)(128)(4,1)} %bitcast.193), calls=%async_computation.2 | async-start | bytes 8388608
  226.5 2.1 copy-start.23
  228.6 8.5 %copy-start.8 = (bf16[2048,512]{1,0:T(8,128)(2,1)}, bf16[2048,512]{1,0:T(8,128)(2,1)S(1)}, u32[]{:S(2)}) copy-start(bf16[2048,512]{1,0:T(8,128)(2,1)S(1)} %get-tuple-element.43) | copy-start | bytes 6291460
  228.6 8.9 %copy-start.25 = (bf16[2048,384]{1,0:T(8,128)(2,1)S(1)}, bf16[2048,384]{1,0:T(8,128)(2,1)}, u32[]{:S(2)}) copy-start(bf16[2048,384]{1,0:T(8,128)(2,1)} %get-tuple-element.26) | copy-start | bytes 4718596
  237.5 15.8 %copy-start.2 = (bf16[128,2048]{1,0:T(8,128)(2,1)S(1)}, bf16[128,2048]{1,0:T(8,128)(2,1)}, u32[]{:S(2)}) copy-start(bf16[128,2048]{1,0:T(8,128)(2,1)} %x_ref.1) | copy-start | bytes 1572868
  237.5 15.9 %copy-start.11 = (f32[16,128,128]{2,1,0:T(8,128)S(1)}, f32[16,128,128]{2,1,0:T(8,128)}, u32[]{:S(2)}) copy-start(f32[16,128,128]{2,1,0:T(8,128)} %copy-done.10) | copy-start | bytes 3145732
  237.5 15.9 %copy-start.15 = (bf16[16,128,1,1,128]{4,1,0,3,2:T(8,128)(2,1)S(1)}, bf16[16,128,1,1,128]{4,1,0,3,2:T(8,128)(2,1)}, u32[]{:S(2)}) copy-start(bf16[16,128,1,1,128]{4,1,0,3,2:T(8,128)(2,1)} %copy-done.14) | copy-start | bytes 1572868
  253.2 1.6 copy-start.26
  254.8 9.2 %copy-start.18 = (bf16[640,2048]{1,0:T(8,128)(2,1)S(1)}, bf16[640,2048]{1,0:T(8,128)(2,1)}, u32[]{:S(2)}) copy-start(bf16[640,2048]{1,0:T(8,128)(2,1)} %copy-done.17) | copy-start | bytes 7864324
  494.3 2.6 copy-start.4
  494.4 2.6 copy-start.9
  494.4 2.6 copy-start.12
  494.4 2.6 copy-start.20
  501.8 9.0 %copy-start.5 = (bf16[128,8192]{1,0:T(8,128)(2,1)S(1)}, bf16[128,8192]{1,0:T(8,128)(2,1)}, u32[]{:S(2)}) copy-start(bf16[128,8192]{1,0:T(8,128)(2,1)} %get-tuple-element.33) | copy-start | bytes 6291460
  514.6 1.9 copy-start.22
Sparse Core Ops, SparseCore 0:
  253.3 135.5 all-reduce.2

commit v3 on v0

--- a/solution.py
+++ b/solution.py
@@ -1,6 +1,11 @@
+import functools
+
 import jax
 import jax.numpy as jnp
+import numpy as np
 from jax import lax
+from jax.experimental import pallas as pl
+from jax.experimental.pallas import tpu as pltpu
 from jax.sharding import PartitionSpec as P
 
 D = 2048
@@ -322,7 +327,888 @@
     )
 
 
+MESH = pl.DeviceIdType.MESH
+bf = jnp.bfloat16
+f32 = jnp.float32
+WIDE = 2048
+TOK = 2048
+
+
+def ds(start, size):
+    return pl.ds(pl.multiple_of(start, size), size)
+
+
+def mm(a, b, ca, cb):
+    return lax.dot_general(a, b, (((ca,), (cb,)), ((), ())), preferred_element_type=f32)
+
+
+def layer_kernel(
+    x_ref, bg_ref, sm_ref, jw_ref, ew_ref, wo_ref, ws_ref, ct_ref, st_ref, eb_ref,
+    SO1, SO2, OSo, JWo, EWo, FIN, SMO,
+    X, BG, WJ, WE, WOS, INNER, QKV, SLOPE, CT, ST, PR, L1, RING, A1, B1, C1, C2X,
+    JB, RX, OSB, ROS, STAGE, T1, SM, SMF, CV, GBR, COL, VC, VEC, VR, TOT, TX, BSUM,
+    su, sd, sy, ss, rx_, bu, bd, by, bs, rb_, sw, rw, sxw, rxw, ssm, rsm,
+    sa, ra, sbb, rbb, sc, rc_, sx, rxx, so, ro, so2, ro2, sg, rg, sf, rf, sv, rv, st_, rt_, lsem, ready,
+):
+    r = lax.axis_index("rep")
+    f = lax.axis_index("fsdp")
+    z = f // 4
+    y = (f // 2) % 2
+    c = f % 2
+    sib = (r, z * 4 + y * 2 + (1 - c))
+    yo = z * 4 + (1 - y) * 2 + c
+    yp = (r, yo)
+    xp = (1 - r, f)
+    lower = z <= 1
+    zz = jnp.where(lower, z, 3 - z)
+
+    def phys(q):
+        return jnp.where(lower, q, 3 - q)
+
+    f_in = (r, jnp.where(lower, f + 4, f - 4))
+    f_out = (r, jnp.where(lower, f - 4, f + 4))
+
+    barrier = pltpu.get_barrier_semaphore()
+
+    @pl.loop(1, 16)
+    def _(k):
+        pl.semaphore_signal(barrier, inc=1, device_id=(r, (f + k) % 16), device_id_type=MESH)
+
+    pl.semaphore_signal(barrier, inc=1, device_id=xp, device_id_type=MESH)
+    pl.semaphore_wait(barrier, 16)
+
+    def rc(src, dst, s, q, dev):
+        return pltpu.make_async_remote_copy(
+            src_ref=src, dst_ref=dst, send_sem=s, recv_sem=q, device_id=dev, device_id_type=MESH
+        )
+
+    def lc(src, dst, s):
+        return pltpu.make_async_copy(src, dst, s)
+
+    def gather(own, OUT, su, sd, sy, ss, rr):
+        def item(i):
+            return OUT.at[ds(128 * i, 128)]
+
+        def up(i, src=None):
+            return rc(item(i) if src is None else src, item(i), su.at[i], rr.at[i], (r, f + 4))
+
+        def dn(i, src=None):
+            return rc(item(i) if src is None else src, item(i), sd.at[i], rr.at[i], (r, f - 4))
+
+        def ac(i, src=None):
+            return rc(item(i) if src is None else src, item(i), sy.at[i], rr.at[i], yp)
+
+        def sb(i, src=None):
+            return rc(item(i) if src is None else src, item(i), ss.at[i], rr.at[i], sib)
+
+        def begin():
+            pl.when(z < 3)(lambda: up(f, own).start())
+            pl.when(z > 0)(lambda: dn(f, own).start())
+            ac(f, own).start()
+            sb(f, own).start()
+
+        def step(s):
+            @pl.when(z - s >= 0)
+            def _():
+                i = f - 4 * s
+                up(i).wait_recv()
+                pl.when(z < 3)(lambda: up(i).start())
+                ac(i).start()
+                sb(i).start()
+
+            @pl.when(z + s <= 3)
+            def _():
+                i = f + 4 * s
+                dn(i).wait_recv()
+                pl.when(z > 0)(lambda: dn(i).start())
+                ac(i).start()
+                sb(i).start()
+
+        def ystep(s):
+            if s == 0:
+                ac(yo).wait_recv()
+                sb(yo).start()
+            else:
+                @pl.when(z - s >= 0)
+                def _():
+                    ac(yo - 4 * s).wait_recv()
+                    sb(yo - 4 * s).start()
+
+                @pl.when(z + s <= 3)
+                def _():
+                    ac(yo + 4 * s).wait_recv()
+                    sb(yo + 4 * s).start()
+
+        def finish():
+            @pl.loop(0, 8)
+            def _(k):
+                sb(2 * k + (1 - c)).wait_recv()
+
+            @pl.loop(0, 8)
+            def _(k):
+                sb(2 * k + c).wait_send()
+
+            @pl.loop(0, 4)
+            def _(k):
+                i = k * 4 + y * 2 + c
+                ac(i).wait_send()
+                pl.when((k <= z) & (z < 3))(lambda: up(i).wait_send())
+                pl.when((k >= z) & (z > 0))(lambda: dn(i).wait_send())
+
+        return begin, step, ystep, finish
+
+    xb, xs, xy, xf = gather(x_ref, X, su, sd, sy, ss, rx_)
+    gb, gs, gy, gf = gather(bg_ref, BG, bu, bd, by, bs, rb_)
+
+    def wpieces(src, dst, from_arg):
+        rows = ds(128 * src + 64 * r, 64)
+        out = []
+        for t in range(3):
+            d = WJ.at[rows, pl.ds(128 * t, 128)]
+            out.append((jw_ref.at[ds(64 * r, 64), ds(2048 * t + 128 * dst, 128)] if from_arg else d, d))
+        d = WE.at[rows]
+        out.append((ew_ref.at[ds(64 * r, 64), ds(512 * dst, 512)] if from_arg else d, d))
+        return out
+
+    def fwd(lo, hi):
+        @pl.loop(lo, hi)
+        def _(k):
+            fs = (f + 16 - k) % 16
+            for t, (s, d) in enumerate(wpieces(fs, f, False)):
+                rc(s, d, sw.at[fs, t], rw.at[fs, t], (r, f)).wait_recv()
+                rc(s, d, sxw.at[fs, t], rxw.at[fs, t], xp).start()
+
+    own_x = lc(x_ref, X.at[ds(128 * f, 128)], lsem.at[0])
+    own_b = lc(bg_ref, BG.at[ds(128 * f, 128)], lsem.at[1])
+    load_o = lc(wo_ref, WOS.at[pl.ds(0, 128)], lsem.at[2])
+    load_s = lc(ws_ref, WOS.at[pl.ds(128, 512)], lsem.at[3])
+    own_s = lc(sm_ref, SM.at[f], lsem.at[4])
+    xb()
+    for cp in (own_x, own_b, load_o, load_s, own_s):
+        cp.start()
+
+    @pl.loop(1, 16)
+    def _(k):
+        fd = (f + k) % 16
+        rc(sm_ref, SM.at[f], ssm.at[fd], rsm.at[f], (r, fd)).start()
+        for t, (s, d) in enumerate(wpieces(f, fd, True)):
+            rc(s, d, sw.at[fd, t], rw.at[f, t], (r, fd)).start()
+
+    for t, (s, d) in enumerate(wpieces(f, f, True)):
+        rc(s, d, sxw.at[f, t], rxw.at[f, t], xp).start()
+        lc(s, d, rw.at[f, t]).start()
+    xs(1)
+    xy(0)
+    fwd(1, 5)
+    xs(2)
+    xy(1)
+    fwd(5, 9)
+    xs(3)
+    xy(2)
+    fwd(9, 13)
+    gb()
+    xy(3)
+    own_s.wait()
+
+    @pl.loop(1, 16)
+    def _(k):
+        fs = (f + k) % 16
+        other = rc(sm_ref, SM.at[fs], ssm.at[fs], rsm.at[fs], (r, fs))
+        other.wait_recv()
+        other.wait_send()
+
+    @pl.loop(0, 16)
+    def _(i):
+        SMF[ds(16 * i, 16)] = SM[i].astype(f32)
+
+    send_small = lc(SMF, SMO, lsem.at[4])
+    send_small.start()
+
+    @pl.loop(0, 16)
+    def _(i):
+        rows = ds(128 * i, 128)
+        place = jnp.broadcast_to(SMF[pl.ds(16 * i + 10, 1)], (128, 128)).T
+        pick = (place == lax.broadcasted_iota(jnp.int32, (128, 128), 1).astype(f32)).astype(f32)
+        hi = lax.Precision.HIGHEST
+        CT[rows] = jnp.dot(pick, ct_ref[...], precision=hi, preferred_element_type=f32)
+        ST[rows] = jnp.dot(pick, st_ref[...], precision=hi, preferred_element_type=f32)
+
+    fwd(13, 16)
+    own_x.wait()
+    xf()
+
+    @pl.loop(0, 16)
+    def _(i):
+        @pl.loop(0, 8, unroll=2)
+        def _(k):
+            w = ds(128 * i + 16 * k, 16)
+            v = X[w].astype(f32)
+            v = v - jnp.mean(v, -1, keepdims=True)
+            v = v * lax.rsqrt(jnp.mean(v * v, -1, keepdims=True) + epsilon)
+            X[w] = v.astype(bf)
+
+        @pl.when(i == 8)
+        def _():
+            gs(1)
+            gy(0)
+
+    gs(2)
+    gy(1)
+
+    for t, (s, d) in enumerate(wpieces(f, f, True)):
+        lc(s, d, rw.at[f, t]).wait()
+    other_half = lambda src: ds(128 * src + 64 * (1 - r), 64)
+
+    @pl.loop(0, 16)
+    def _(fs):
+        for t in range(4):
+            d = WJ.at[other_half(fs), pl.ds(128 * t, 128)] if t < 3 else WE.at[other_half(fs)]
+            cp = rc(d, d, sxw.at[fs, t], rxw.at[fs, t], xp)
+            cp.wait_recv()
+            cp.wait_send()
+
+    load_o.wait()
+    load_s.wait()
+
+    def columns(j):
+        for v in range(4):
+            COL[v] = jnp.broadcast_to(SMF[pl.ds(16 * j + v, 1)], (128, 128)).T
+
+    def fold(v):
+        return v[:8] + v[8:]
+
+    CV[...] = jnp.zeros_like(CV)
+
+    @pl.loop(0, 16)
+    def _(j):
+        columns(j)
+
+        @pl.loop(0, 8)
+        def _(k):
+            w = ds(128 * j + 16 * k, 16)
+            cw = ds(16 * k, 16)
+            g1, s1, g2, s2 = (COL[v, cw] for v in range(4))
+            for t in range(3):
+                l = pl.ds(128 * t, 128)
+                v = WJ[w, l].astype(f32)
+                CV[:, l] += fold(v * s1)
+                WJ[w, l] = (v * g1).astype(bf)
+            for t in range(4):
+                l = pl.ds(128 * t, 128)
+                lo = pl.ds(384 + 128 * t, 128)
+                v = WE[w, l].astype(f32)
+                CV[:, lo] += fold(v * s2)
+                WE[w, l] = (v * g2).astype(bf)
+
+    CV[...] = jnp.broadcast_to(jnp.sum(CV[...], 0, keepdims=True), CV.shape)
+    for t in range(3):
+        place = (16 * t + f) // 3 * 16 + 6 + (16 * t + f) % 3
+        CV[:, pl.ds(128 * t, 128)] += SMF[pl.ds(place, 1)]
+    CV[:, pl.ds(384, 512)] += eb_ref[...]
+
+    lane = lax.broadcasted_iota(jnp.int32, (16, 128), 1)
+
+    def swap(v, ln):
+        return jnp.where(ln < 16, pltpu.roll(v, 112, 1), pltpu.roll(v, 16, 1))
+
+    @pl.loop(0, 4)
+    def _(i):
+        rows = ds(512 * i, 512)
+        T1[:, pl.ds(0, 384)] = mm(X[rows], WJ[...], 1, 0)
+        T1[:, pl.ds(384, 512)] = mm(X[rows], WE[...], 1, 0)
+
+        @pl.loop(0, 32, unroll=2)
+        def _(k):
+            w = ds(16 * k, 16)
+            gw = ds(512 * i + 16 * k, 16)
+            cos, sin = CT[gw], ST[gw]
+            for t in range(2):
+                l = pl.ds(128 * t, 128)
+                v = T1[w, l] + CV[0:1, l]
+                QKV[gw, l] = (v * cos + swap(v, lane) * sin).astype(bf)
+            l = pl.ds(256, 128)
+            QKV[gw, l] = (T1[w, l] + CV[0:1, l]).astype(bf)
+            for t in range(4):
+                l = pl.ds(384 + 128 * t, 128)
+                v = T1[w, l] + CV[0:1, l]
+                part = 0.5 * (1.0 + lax.erf(v * 0.7071067811865476))
+                INNER[gw, pl.ds(128 + 128 * t, 128)] = (v * part).astype(bf)
+                SLOPE[gw, pl.ds(128 * t, 128)] = (
+                    part + v * jnp.exp(-0.5 * v * v) * 0.3989422804014327
+                ).astype(bf)
+
+        @pl.when(i == 1)
+        def _():
+            gs(3)
+            gy(2)
+
+        @pl.when(i == 3)
+        def _():
+            gy(3)
+
+    scale = HEAD_DIM ** (-0.5)
+    down = lax.broadcasted_iota(jnp.int32, (128, 128), 0)
+    across = lax.broadcasted_iota(jnp.int32, (128, 128), 1)
+
+    @pl.loop(0, 16, unroll=2)
+    def _(i):
+        rows = ds(128 * i, 128)
+        q = QKV[rows, pl.ds(0, 128)]
+        k = QKV[rows, pl.ds(128, 128)]
+        v = QKV[rows, pl.ds(256, 128)]
+        seg = jnp.broadcast_to(SMF[pl.ds(16 * i + 9, 1)], (128, 128))
+        s = mm(q, k, 1, 1) * scale
+        s = jnp.where((seg == seg.T) & (across <= down), s, masked_score)
+        e = jnp.exp(s - jnp.max(s, -1, keepdims=True))
+        p = e / jnp.sum(e, -1, keepdims=True)
+        PR[rows] = p
+        INNER[rows, pl.ds(0, 128)] = mm(p.astype(bf), v, 1, 0).astype(bf)
+
+    def add_into(dst, src, rows):
+        @pl.loop(0, rows // 16)
+        def _(i):
+            w = ds(i * 16, 16)
+            dst[w] = (dst[w].astype(f32) + src[w].astype(f32)).astype(bf)
+
+    def reducer(n, sent, own, AA, BB, CC, CX, SO):
+        def a_send(k):
+            return rc(sent(k), AA(k), sa.at[n, k], ra.at[n, k], sib)
+
+        def b_send(zp):
+            return rc(own(zp * 2 + 1 - y), BB(zp), sbb.at[n, zp], rbb.at[n, zp], yp)
+
+        def prep(k):
+            a_send(k).wait_recv()
+            add_into(own(k), AA(k), 128)
+
+        def far():
+            for q in (3, 0, 2, 1):
+                prep(phys(q) * 2 + 1 - y)
+                b_send(phys(q)).start()
+
+        def near(q):
+            zp = phys(q)
+            k = zp * 2 + y
+            prep(k)
+            b_send(zp).wait_recv()
+            add_into(own(k), BB(zp), 128)
+
+        def got(q, extra=False):
+            zp = phys(q)
+            buf = CX if extra else CC(zp)
+            slot = 4 if extra else zp
+            rc(buf, buf, sc.at[n, zp], rc_.at[n, slot], f_in).wait_recv()
+            return buf
+
+        def send(q, dev, extra=False):
+            zp = phys(q)
+            return rc(
+                own(zp * 2 + y), CX if extra else CC(zp), sc.at[n, zp], rc_.at[n, 4 if extra else zp], dev
+            )
+
+        def step(q):
+            near(q)
+            zp = phys(q)
+            k = zp * 2 + y
+
+            @pl.when(zz == 0)
+            def _():
+                if q > 0:
+                    send(q, f_in).start()
+
+            @pl.when(zz == 1)
+            def _():
+                if q >= 2:
+                    add_into(own(k), got(q), 128)
+                    send(q, f_in, q == 2).start()
+                if q == 0:
+                    add_into(own(k), got(q), 128)
+                    send(q, f_out).start()
+
+        def total(q, bufs):
+            k = phys(q) * 2 + y
+
+            @pl.loop(0, 8)
+            def _(i):
+                w = ds(i * 16, 16)
+                v = own(k)[w].astype(f32)
+                for b in bufs:
+                    v = v + b[w].astype(f32)
+                STAGE[w] = v
+
+        def last():
+            @pl.when(zz == 0)
+            def _():
+                total(0, [got(0)])
+
+            @pl.when(zz == 1)
+            def _():
+                total(1, [got(1), got(1, True)])
+
+            cp = lc(STAGE, SO, lsem.at[5])
+            cp.start()
+            cp.wait()
+
+        def drain(first=0):
+            @pl.loop(first, 8)
+            def _(k):
+                a_send(k).wait_send()
+
+            @pl.loop(0, 4)
+            def _(zp):
+                b_send(zp).wait_send()
+
+            for q in range(4):
+                if q > 0:
+                    pl.when(zz == 0)(lambda: send(q, f_in).wait_send())
+                if q >= 2:
+                    pl.when(zz == 1)(lambda: send(q, f_in, q == 2).wait_send())
+                if q == 0:
+                    pl.when(zz == 1)(lambda: send(q, f_out).wait_send())
+
+        return a_send, far, step, last, drain
+
+    R1 = reducer(
+        0, lambda k: RING.at[k % 3], lambda k: L1.at[k], lambda k: A1.at[k], lambda k: B1.at[k],
+        lambda k: C1.at[k], C1.at[4], SO1,
+    )
+    R2 = reducer(
+        1,
+        lambda k: BG.at[ds(128 * (2 * k + 1 - c), 128)],
+        lambda k: BG.at[ds(128 * (2 * k + c), 128)],
+        lambda k: X.at[ds(128 * k, 128)],
+        lambda k: X.at[ds(1024 + 128 * k, 128)],
+        lambda k: X.at[ds(1536 + 128 * k, 128)],
+        C2X,
+        SO2,
+    )
+
+    @pl.loop(0, 8)
+    def _(b):
+        res = mm(INNER[ds(256 * b, 256)], WOS[...], 1, 0)
+
+        @pl.when(b >= 3)
+        def _():
+            R1[0](b - 3).wait_send()
+
+        for side in range(2):
+            @pl.when(c == side)
+            def _():
+                L1[b] = res[128 * side : 128 * side + 128].astype(bf)
+                RING[b % 3] = res[128 - 128 * side : 256 - 128 * side].astype(bf)
+
+        R1[0](b).start()
+
+    own_b.wait()
+    gf()
+
+    half = ds(320 * r, 320)
+    away = ds(320 * (1 - r), 320)
+
+    def o1(j):
+        return rc(OSB.at[j, away], ROS.at[j], so.at[j], ro.at[j], xp)
+
+    def o2(j):
+        return rc(OSB.at[j, half], OSo.at[half, ds(512 * j, 512)], so2.at[j], ro2.at[j], xp)
+
+    def o2r(j):
+        return rc(OSB.at[j, half], OSo.at[away, ds(512 * j, 512)], so2.at[j], ro2.at[j], xp)
+
+    def os_store(j):
+        return lc(OSB.at[j, half], OSo.at[half, ds(512 * j, 512)], lsem.at[6 + j])
+
+    def os_step(j):
+        o1(j).wait_recv()
+        add_into(OSB.at[j, half], ROS.at[j], 320)
+        o2(j).start()
+        os_store(j).start()
+
+    def os_drain():
+        for j in range(4):
+            o1(j).wait_send()
+            o2(j).wait_send()
+            o2r(j).wait_recv()
+            os_store(j).wait()
+
+    @pl.loop(0, 4)
+    def _(j):
+        OSB[j] = mm(INNER[...], BG[:, ds(512 * j, 512)], 0, 0).astype(bf)
+        o1(j).start()
+
+    R1[1]()
+
+    GBR[...] = jnp.zeros_like(GBR)
+    VEC[...] = jnp.zeros_like(VEC)
+    TOT[...] = jnp.zeros_like(TOT)
+    mine = BG[:, ds(128 * f, 128)].astype(f32)
+    BSUM[...] = jnp.sum(mine, 0, keepdims=True)
+
+    def fold_rows(v, rows):
+        return jnp.sum(v.reshape(rows // 8, 8, v.shape[-1]), 0)
+
+    @pl.loop(0, 4)
+    def _(i):
+        rows = ds(512 * i, 512)
+        T1[:, pl.ds(0, 640)] = mm(BG[rows], WOS[...], 1, 1)
+
+        @pl.loop(0, 32, unroll=2)
+        def _(k):
+            w = ds(16 * k, 16)
+            gw = ds(512 * i + 16 * k, 16)
+            INNER[gw, pl.ds(0, 128)] = T1[w, pl.ds(0, 128)].astype(bf)
+            e = (T1[w, pl.ds(128, 512)] * SLOPE[gw].astype(f32)).astype(bf)
+            SLOPE[gw] = e
+            GBR[:, pl.ds(384, 512)] += fold(e.astype(f32))
+
+    os_step(0)
+    R1[2](3)
+    os_step(1)
+    R1[2](0)
+
+    lane_b = lax.broadcasted_iota(jnp.int32, (128, 128), 1)
+
+    @pl.loop(0, 16, unroll=2)
+    def _(i):
+        rows = ds(128 * i, 128)
+        q = QKV[rows, pl.ds(0, 128)]
+        k = QKV[rows, pl.ds(128, 128)]
+        v = QKV[rows, pl.ds(256, 128)]
+        p = PR[rows]
+        mg = INNER[rows, pl.ds(0, 128)]
+        vg = mm(p.astype(bf), mg, 0, 0)
+        pg = mm(mg, v, 1, 1)
+        sgr = (p * (pg - jnp.sum(pg * p, -1, keepdims=True))).astype(bf)
+        cos, sin = CT[rows], ST[rows]
+        qg = mm(sgr, k, 1, 0) * scale
+        kg = mm(sgr, q, 0, 0) * scale
+        for t, g in enumerate((qg, kg, vg)):
+            if t < 2:
+                g = g * cos - swap(g, lane_b) * sin
+            g = g.astype(bf)
+            l = pl.ds(128 * t, 128)
+            QKV[rows, l] = g
+            GBR[:, l] += fold_rows(g.astype(f32), 128)
+
+    os_step(2)
+    R1[2](2)
+    os_step(3)
+    R1[2](1)
+    GBR[...] = jnp.broadcast_to(jnp.sum(GBR[...], 0, keepdims=True), GBR.shape)
+
+    keep = ds(64 * r, 64)
+    give = ds(64 * (1 - r), 64)
+
+    def x1(g):
+        return rc(JB.at[ds(4 * g, 4), give], RX.at[ds(4 * g, 4)], sx.at[g], rxx.at[g], xp)
+
+    def place_of(fs, t, rows):
+        if t < 3:
+            return JWo.at[rows, ds(2048 * t + 128 * fs, 128)]
+        return EWo.at[rows, ds(512 * fs, 512)]
+
+    def piece_of(fd, t):
+        return JB.at[fd, keep, pl.ds(128 * t, 128)] if t < 3 else JB.at[fd, keep, pl.ds(384, 512)]
+
+    def je_group(g):
+        x1(g).wait_recv()
+
+        @pl.loop(0, 4)
+        def _(j):
+            fd = 4 * g + j
+            add_into(JB.at[fd, keep], RX.at[fd], 64)
+
+            @pl.when(fd != f)
+            def _():
+                for t in range(4):
+                    rc(piece_of(fd, t), place_of(f, t, keep), sg.at[fd, t], rg.at[f, t], (r, fd)).start()
+
+            @pl.when(fd == f)
+            def _():
+                for t in range(4):
+                    lc(piece_of(fd, t), place_of(f, t, keep), sg.at[fd, t]).start()
+                    rc(piece_of(fd, t), place_of(f, t, keep), sf.at[fd, t], rf.at[f, t], xp).start()
+
+    def fwd_group(g):
+        @pl.loop(4 * g, 4 * g + 4)
+        def _(fs):
+            @pl.when(fs != f)
+            def _():
+                for t in range(4):
+                    d = place_of(fs, t, keep)
+                    rc(d, d, sg.at[fs, t], rg.at[fs, t], xp).wait_recv()
+                    rc(d, d, sf.at[fs, t], rf.at[fs, t], xp).start()
+
+    def je_drain():
+        for g in range(4):
+            x1(g).wait_send()
+
+        @pl.loop(0, 16)
+        def _(fs):
+            for t in range(4):
+                d = place_of(fs, t, give)
+                cp = rc(d, d, sf.at[fs, t], rf.at[fs, t], xp)
+                cp.wait_recv()
+                cp.wait_send()
+
+            @pl.when(fs != f)
+            def _():
+                for t in range(4):
+                    rc(piece_of(fs, t), place_of(f, t, keep), sg.at[fs, t], rg.at[f, t], xp).wait_send()
+
+            @pl.when(fs == f)
+            def _():
+                for t in range(4):
+                    lc(piece_of(fs, t), place_of(f, t, keep), sg.at[fs, t]).wait()
+
+    @pl.loop(0, 4)
+    def _(i):
+        left = X[:, ds(512 * i, 512)]
+        T1[:, pl.ds(0, 384)] = mm(left, QKV[...], 0, 0)
+        T1[:, pl.ds(384, 512)] = mm(left, SLOPE[...], 0, 0)
+
+        @pl.loop(0, 4)
+        def _(s):
+            j = 4 * i + s
+            columns(j)
+
+            @pl.loop(0, 8)
+            def _(k):
+                w = ds(128 * s + 16 * k, 16)
+                gw = ds(128 * j + 16 * k, 16)
+                cw = ds(16 * k, 16)
+                for b, (first, count, W) in enumerate(((0, 3, WJ), (384, 4, WE))):
+                    g, sh = COL[2 * b, cw], COL[2 * b + 1, cw]
+                    a1 = jnp.zeros((16, 128), f32)
+                    a2 = jnp.zeros((16, 128), f32)
+                    for t in range(count):
+                        l = pl.ds(first + 128 * t, 128)
+                        m = T1[w, l]
+                        bias = GBR[0:1, l]
+                        JB[j, cw, l] = (g * m + sh * bias).astype(bf)
+                        wt = W[gw, pl.ds(128 * t, 128)].astype(f32)
+                        a1 = a1 + wt * m
+                        a2 = a2 + wt * bias
+                    VC[2 * b, cw] = jnp.sum(a1, -1, keepdims=True) / g
+                    VC[2 * b + 1, cw] = jnp.sum(a2, -1, keepdims=True) / g
+
+            for v in range(4):
+                VEC[j, pl.ds(v, 1)] = VC[v].T[0:1]
+
+        x1(i).start()
+
+    def tile(fd, src):
+        return rc(VEC.at[fd], VR.at[src], sv.at[fd], rv.at[src], (r, fd))
+
+    for t in range(3):
+        VEC[(16 * t + f) // 3, pl.ds(4 + (16 * t + f) % 3, 1)] = GBR[0:1, pl.ds(128 * t, 128)]
+    TOT[pl.ds(7, 1)] = BSUM[...]
+    for t in range(4):
+        TOT[pl.ds(8 + t, 1)] = GBR[0:1, pl.ds(384 + 128 * t, 128)]
+
+    @pl.loop(1, 16)
+    def _(k):
+        tile((f + k) % 16, f).start()
+
+    VR[f] = VEC[f]
+    R1[3]()
+
+    for dev in (sib, yp, f_in):
+        pl.semaphore_signal(ready, inc=1, device_id=dev, device_id_type=MESH)
+
+    @pl.when(zz == 1)
+    def _():
+        pl.semaphore_signal(ready, inc=1, device_id=f_out, device_id_type=MESH)
+        pl.semaphore_wait(ready, 4)
+
+    @pl.when(zz == 0)
+    def _():
+        pl.semaphore_wait(ready, 3)
+
+    @pl.loop(0, 8)
+    def _(b):
+        rows = ds(256 * b, 256)
+        BG[rows] = (mm(QKV[rows], WJ[...], 1, 1) + mm(SLOPE[rows], WE[...], 1, 1)).astype(bf)
+        R2[0](b).start()
+
+    def total_rep():
+        return rc(TOT, TX, st_, rt_, xp)
+
+    @pl.loop(1, 16)
+    def _(k):
+        tile(f, (f + k) % 16).wait_recv()
+
+    TOT[pl.ds(0, 7)] = jnp.sum(VR[...], 0)[0:7]
+    total_rep().start()
+    je_group(0)
+    je_group(1)
+    R2[1]()
+    je_group(2)
+    je_group(3)
+    R2[2](3)
+    fwd_group(0)
+    R2[2](0)
+    fwd_group(1)
+    R2[2](2)
+    fwd_group(2)
+    R2[2](1)
+    fwd_group(3)
+    R2[3]()
+    R1[4](5)
+    R2[4]()
+    send_small.wait()
+
+    @pl.loop(1, 16)
+    def _(k):
+        fd = (f + k) % 16
+        for t, (s, d) in enumerate(wpieces(f, fd, True)):
+            rc(s, d, sw.at[fd, t], rw.at[f, t], (r, fd)).wait_send()
+
+    @pl.loop(1, 16)
+    def _(k):
+        tile((f + k) % 16, f).wait_send()
+
+    total_rep().wait_recv()
+    total_rep().wait_send()
+    FIN[...] = TOT[...] + TX[...]
+    os_drain()
+    je_drain()
+
+
+def layer_call(x, bg, sm, jw, ew, wo, ws, ct, st, eb):
+    S = jax.ShapeDtypeStruct
+    D = pltpu.SemaphoreType.DMA
+    V = pltpu.VMEM
+    hbm = pl.BlockSpec(memory_space=pl.ANY)
+    vm = pl.BlockSpec(memory_space=pltpu.VMEM)
+    return pl.pallas_call(
+        layer_kernel,
+        out_shape=(
+            S((128, WIDE), f32), S((128, WIDE), f32), S((640, WIDE), bf), S((128, 3 * WIDE), bf),
+            S((128, 4 * WIDE), bf), S((16, 128), f32), S((256, 128), f32),
+        ),
+        in_specs=[hbm] * 7 + [vm] * 3,
+        out_specs=(hbm, hbm, hbm, hbm, hbm, vm, hbm),
+        scratch_shapes=[
+            V((TOK, WIDE), bf), V((TOK, WIDE), bf), V((WIDE, 384), bf), V((WIDE, 512), bf), V((640, WIDE), bf),
+            V((TOK, 640), bf), V((TOK, 384), bf), V((TOK, 512), bf), V((TOK, 128), f32), V((TOK, 128), f32),
+            V((TOK, 128), f32), V((8, 128, WIDE), bf), V((3, 128, WIDE), bf), V((8, 128, WIDE), bf),
+            V((4, 128, WIDE), bf), V((5, 128, WIDE), bf), V((128, WIDE), bf),
+            V((16, 128, 896), bf), V((16, 64, 896), bf), V((4, 640, 512), bf), V((4, 320, 512), bf),
+            V((128, WIDE), f32), V((512, 896), f32), V((16, 16, 128), bf), V((256, 128), f32),
+            V((8, 896), f32), V((8, 896), f32), V((4, 128, 128), f32), V((4, 128, 128), f32),
+            V((16, 8, 128), f32), V((16, 8, 128), f32), V((16, 128), f32), V((16, 128), f32), V((1, 128), f32),
+        ]
+        + [D((16,))] * 10 + [D((16, 4))] * 4 + [D((16,))] * 2
+        + [D((2, 8))] * 2 + [D((2, 4))] * 3 + [D((2, 5))] + [D((4,))] * 6 + [D((16, 4))] * 4
+        + [D((16,))] * 2 + [D, D] + [D((12,)), pltpu.SemaphoreType.REGULAR],
+        compiler_params=pltpu.CompilerParams(
+            collective_id=0, has_side_effects=True, vmem_limit_bytes=67043328
+        ),
+    )(x, bg, sm, jw, ew, wo, ws, ct, st, eb)
+
+
+def wide(a):
+    return a.astype(f32)
+
+
+def turn_tables(length):
+    place = np.arange(length, dtype=np.float32)[:, None]
+    power = np.arange(ROT // 2, dtype=np.float32) * np.float32(2.0) / np.float32(ROT)
+    angle = place * np.power(np.float32(rotary_base), -power)
+    cosine, sine = (np.cos(angle), np.sin(angle))
+    rest = HEAD_DIM - ROT
+    ct = np.concatenate([cosine, cosine, np.ones((length, rest))], 1)
+    st = np.concatenate([-sine, sine, np.zeros((length, rest))], 1)
+    return (jnp.asarray(ct, f32), jnp.asarray(st, f32))
+
+
+def head_body(
+    n,
+    layer_input,
+    segment,
+    live_mask,
+    attention_gain,
+    attention_shift,
+    joined_weight,
+    joined_bias,
+    output_weight,
+    output_bias,
+    feedforward_gain,
+    feedforward_shift,
+    expand_weight,
+    expand_bias,
+    shrink_weight,
+    shrink_bias,
+    cotangent,
+):
+    own, width = layer_input.shape
+    part = width // n
+    live_rows = wide(live_mask[0])[:, None]
+    seeds = wide(cotangent)
+    branch_own = (live_rows * seeds).astype(bf)
+    seg = segment[0]
+    places = jnp.arange(own, dtype=jnp.int32)
+    earlier = jnp.sum((seg[None, :] < seg[:, None]).astype(jnp.int32), -1)
+    lines = (
+        attention_gain.reshape(1, part),
+        attention_shift.reshape(1, part),
+        feedforward_gain.reshape(1, part),
+        feedforward_shift.reshape(1, part),
+        output_bias.reshape(1, part),
+        shrink_bias.reshape(1, part),
+        joined_bias.reshape(3, part),
+        segment.astype(bf),
+        (places - earlier).astype(bf).reshape(1, own),
+    )
+    row = lax.broadcasted_iota(jnp.int32, (16, 128), 0)
+    small = jnp.zeros((16, 128), bf)
+    at = 0
+    for item in lines:
+        for k in range(item.shape[0]):
+            small = jnp.where(row == at, item[k : k + 1], small)
+            at += 1
+    ct, st = turn_tables(own)
+    summed, hat_own, os_grad, joined_grad, expand_grad, sums, small_all = layer_call(
+        layer_input, branch_own, small, joined_weight, expand_weight, output_weight, shrink_weight,
+        ct, st, wide(expand_bias).reshape(1, -1),
+    )
+    small_all = small_all.reshape(n, 16, part)
+    bias = (small_all[:, 4] + small_all[:, 5]).reshape(width)
+    rows_own = wide(layer_input)
+    layer_output = (rows_own + live_rows * (summed + bias)).astype(bf)
+    centred = rows_own - jnp.mean(rows_own, -1, keepdims=True)
+    inverse = lax.rsqrt(jnp.mean(centred * centred, -1, keepdims=True) + epsilon)
+    normalized = centred * inverse
+    row_grad = inverse * (
+        hat_own
+        - jnp.mean(hat_own, -1, keepdims=True)
+        - normalized * jnp.mean(hat_own * normalized, -1, keepdims=True)
+    )
+    input_grad = (seeds + row_grad).astype(bf)
+
+    os_grad = wide(os_grad)
+    return (
+        layer_output,
+        input_grad,
+        sums[0],
+        sums[1],
+        wide(joined_grad),
+        sums[4:7].reshape(-1),
+        os_grad[:part],
+        sums[7],
+        sums[2],
+        sums[3],
+        wide(expand_grad),
+        sums[8:12].reshape(-1),
+        os_grad[part:],
+        sums[7],
+    )
+
+
 def solution(mesh):
+    n = mesh.shape["fsdp"]
+    fits = n == HEADS and mesh.shape["rep"] == 2
+    chosen = functools.partial(head_body, n) if fits else body
     placed = (
         P(("rep", "fsdp"), None),
         P(("rep", "fsdp"), None),
@@ -342,7 +1228,7 @@
         P(("rep", "fsdp"), None),
     )
     return jax.shard_map(
-        body,
+        chosen,
         mesh=mesh,
         in_specs=placed,
         out_specs=(

time: 3240 us -> 382 us (0.12)
  waiting for transfers between devices: 2580 us -> 0 us
  Pallas kernels: 0 us -> 346 us
  blocking collectives: 318 us -> 0 us
  matrix products: 229 us -> 0 us
    reduce_scatter x4 -> x0, waiting for transfers between devices: 1830 us -> none  [the longest x1 633 us: body(): lax.psum_scatter(ff_terms[2], 'fsdp', scatter_dimension=0, tiled=True)]
    all_gather x8 -> x0, waiting for transfers between devices: 692 us -> none  [the longest x2 222 us: body(): lax.all_gather(as_sent(lax.optimization_barrier((feedforward_parts, layer...]
    pallas_call x0 -> x1, Pallas kernels: none -> 346 us  [layer_call(): pl.pallas_call(layer_kernel, out_shape=(S((128, WIDE), f32), S((128, WIDE...]
    all_gather x14 -> x0, blocking collectives: 260 us -> none  [the longest x3 55.6 us: body(): lax.all_gather(as_sent(lax.optimization_barrier((attention_parts, layer_o...]
    dot_general x21 -> x0, matrix products: 229 us -> none  [the longest x1 29.9 us: body(): jnp.einsum('tf,td->fd', activated, branch_grad, preferred_element_type=jn...]
    unnamed x1 -> x0, blocking collectives: 53.5 us -> none
    psum x1 -> x0, waiting for transfers between devices: 49.2 us -> none  [body(): lax.psum(at_parts[2].astype(jnp.bfloat16), 'rep').astype(jnp.float32)]
  transfers between devices with their start and end apart: 13 -> 0, of which waited for: 12 -> 0; matrix products, arithmetic and copies ran while one was open for 8% -> 0% of each run, Pallas kernels for 0% -> 0%
where the time goes in v3:
time: 382 us; the launch traced here: 375 us
  Pallas kernels  346 us (91%)
  other arithmetic  19.5 us (5%)
  local copies, waits for them, and re-layouts  8.05 us (2%)
    pallas_call x1, Pallas kernels, layer_call(): pl.pallas_call(layer_kernel, out_shape=(S((128, WIDE), f32), S((128, WIDE...  346 us

profile of v3, /device:TPU:10, one launch (start us, length us, event | category | flops | bytes accessed | tf_op | source)
XLA Modules:
  0.0 374.8 jit_solution(9315785210621904316)
XLA Ops:
  0.6 0.8 fusion.12
  1.5 0.9 convert_reduce_fusion.1
  2.4 0.7 convert_bitcast_fusion
  3.1 1.4 select_select_fusion.sm_ref
  4.5 0.7 convert_bitcast_fusion.1
  5.2 0.0 copy-start.7
  5.2 0.5 copy-done.7
  5.7 2.0 fusion.8.bg_ref
  7.7 1.3 reshape.111
  8.9 346.5 %shard_map.281 = (f32[128,2048]{1,0:T(8,128)}, f32[128,2048]{1,0:T(8,128)}, bf16[640,2048]{1,0:T(8,128)(2,1)}, bf16[128,6144]{1,0:T(8,128)(2,1)}, bf16[128,8192]...) custom-call(bf16[128,2048]{1,0:T(8,128)(2,1)} %x_ref.1, bf16[128,2048]{1,0:T(8,128)(2,1)} %fusion.8.bg_ref, ...), custom_call_target="tpu_custom_call" | custom-call | tf_op jit(solution)/shard_map/pallas_call | solution.py:1083
  355.4 0.0 copy-start
  355.4 0.0 copy-start.2
  355.4 0.0 copy-start.4
  355.4 0.0 copy-start.8
  355.4 1.3 convert_reduce_fusion
  356.8 1.3 fusion.7
  358.1 1.7 fusion.11
  359.8 0.9 slice_add_fusion
  360.8 0.0 copy-done
  360.8 0.0 copy-done.2
  360.8 0.0 copy-done.4
  360.8 0.0 copy-done.8
  360.8 0.0 copy-start.6
  360.8 0.0 copy-start.1
  360.8 2.9 fusion.9
  363.7 0.0 copy-done.6
  363.7 0.5 slice_bitcast_fusion.2
  364.2 0.0 copy-start.9
  364.2 0.6 slice_bitcast_fusion
  364.8 0.6 slice_bitcast_fusion.1
  365.4 0.0 copy-done.1
  365.4 2.5 slice.63
  367.9 0.0 copy-start.3
  367.9 1.1 slice.62
  369.0 0.9 copy-done.3
  369.9 0.0 copy-start.5
  369.9 2.4 convert_element_type.60
  372.3 0.0 copy-done.5
  372.3 2.0 convert_element_type.58
  374.3 0.0 copy-done.9
  374.3 0.5 copy.33
  (11 shorter events, 0.1 us)
Async XLA Ops:
  5.2 0.5 copy-start.7
  355.4 5.4 %copy-start = (bf16[128,2048]{1,0:T(8,128)(2,1)S(1)}, bf16[128,2048]{1,0:T(8,128)(2,1)}, u32[]{:S(2)}) copy-start(bf16[128,2048]{1,0:T(8,128)(2,1)} %x_ref.1) | copy-start | bytes 1572868
  355.4 5.4 %copy-start.2 = (f32[128,2048]{1,0:T(8,128)S(1)}, f32[128,2048]{1,0:T(8,128)}, u32[]{:S(2)}) copy-start(f32[128,2048]{1,0:T(8,128)} %get-tuple-element.23) | copy-start | bytes 3145732
  355.4 5.4 %copy-start.4 = (bf16[128,2048]{1,0:T(8,128)(2,1)S(1)}, bf16[128,2048]{1,0:T(8,128)(2,1)}, u32[]{:S(2)}) copy-start(bf16[128,2048]{1,0:T(8,128)(2,1)} %param.33) | copy-start | bytes 1572868
  355.4 5.4 %copy-start.8 = (f32[128]{0:T(128)S(1)}, f32[128]{0:T(128)}, u32[]{:S(2)}) copy-start(f32[128]{0:T(128)} %copy-done.7) | copy-start | bytes 1540
  360.8 2.9 copy-start.6
  360.8 4.6 %copy-start.1 = (bf16[640,2048]{1,0:T(8,128)(2,1)S(1)}, bf16[640,2048]{1,0:T(8,128)(2,1)}, u32[]{:S(2)}) copy-start(bf16[640,2048]{1,0:T(8,128)(2,1)} %get-tuple-element.26) | copy-start | bytes 7864324
  364.2 10.1 %copy-start.9 = (f32[128]{0:T(128)}, f32[128]{0:T(128)S(1)}, u32[]{:S(2)}) copy-start(f32[128]{0:T(128)S(1)} %get-tuple-element.77) | copy-start | bytes 1540
  367.9 2.0 copy-start.3
  369.9 2.4 copy-start.5

commit v4 on v3

--- a/solution.py
+++ b/solution.py
@@ -343,10 +343,10 @@
 
 
 def layer_kernel(
-    x_ref, bg_ref, sm_ref, jw_ref, ew_ref, wo_ref, ws_ref, ct_ref, st_ref, eb_ref,
+    x_ref, bg_ref, sm_ref, jw_ref, ew_ref, wo_ref, ws_ref, ct_ref, eb_ref,
     SO1, SO2, OSo, JWo, EWo, FIN, SMO,
-    X, BG, WJ, WE, WOS, INNER, QKV, SLOPE, CT, ST, PR, L1, RING, A1, B1, C1, C2X,
-    JB, RX, OSB, ROS, STAGE, T1, SM, SMF, CV, GBR, COL, VC, VEC, VR, TOT, TX, BSUM,
+    X, BG, WJ, WE, WOS, INNER, QKV, SLOPE, CT, PR, L1, RING, A1, B1, C1, A2,
+    JB, RX, OSB, ROS, T1, SM, SMF, CV, GBR, VEC, VR, TOT, TX, BSUM,
     su, sd, sy, ss, rx_, bu, bd, by, bs, rb_, sw, rw, sxw, rxw, ssm, rsm,
     sa, ra, sbb, rbb, sc, rc_, sx, rxx, so, ro, so2, ro2, sg, rg, sf, rf, sv, rv, st_, rt_, lsem, ready,
 ):
@@ -401,9 +401,11 @@
         def sb(i, src=None):
             return rc(item(i) if src is None else src, item(i), ss.at[i], rr.at[i], sib)
 
-        def begin():
+        def begin_z():
             pl.when(z < 3)(lambda: up(f, own).start())
             pl.when(z > 0)(lambda: dn(f, own).start())
+
+        def begin_y():
             ac(f, own).start()
             sb(f, own).start()
 
@@ -425,25 +427,21 @@
                 sb(i).start()
 
         def ystep(s):
-            if s == 0:
-                ac(yo).wait_recv()
-                sb(yo).start()
-            else:
-                @pl.when(z - s >= 0)
-                def _():
-                    ac(yo - 4 * s).wait_recv()
-                    sb(yo - 4 * s).start()
-
-                @pl.when(z + s <= 3)
-                def _():
-                    ac(yo + 4 * s).wait_recv()
-                    sb(yo + 4 * s).start()
+            @pl.when(z - s >= 0)
+            def _():
+                ac(yo - 4 * s).wait_recv()
+                sb(yo - 4 * s).start()
+
+            @pl.when((s > 0) & (z + s <= 3))
+            def _():
+                ac(yo + 4 * s).wait_recv()
+                sb(yo + 4 * s).start()
+
+        def landed(q):
+            for v in range(2):
+                sb(4 * q + 2 * v + 1 - c).wait_recv()
 
         def finish():
-            @pl.loop(0, 8)
-            def _(k):
-                sb(2 * k + (1 - c)).wait_recv()
-
             @pl.loop(0, 8)
             def _(k):
                 sb(2 * k + c).wait_send()
@@ -455,10 +453,10 @@
                 pl.when((k <= z) & (z < 3))(lambda: up(i).wait_send())
                 pl.when((k >= z) & (z > 0))(lambda: dn(i).wait_send())
 
-        return begin, step, ystep, finish
-
-    xb, xs, xy, xf = gather(x_ref, X, su, sd, sy, ss, rx_)
-    gb, gs, gy, gf = gather(bg_ref, BG, bu, bd, by, bs, rb_)
+        return begin_z, begin_y, step, ystep, landed, finish
+
+    xz, xo, xs, xy, xl, xf = gather(x_ref, X, su, sd, sy, ss, rx_)
+    gz, go, gs, gy, gl, gf = gather(bg_ref, BG, bu, bd, by, bs, rb_)
 
     def wpieces(src, dst, from_arg):
         rows = ds(128 * src + 64 * r, 64)
@@ -483,31 +481,33 @@
     load_o = lc(wo_ref, WOS.at[pl.ds(0, 128)], lsem.at[2])
     load_s = lc(ws_ref, WOS.at[pl.ds(128, 512)], lsem.at[3])
     own_s = lc(sm_ref, SM.at[f], lsem.at[4])
-    xb()
+    def wsend(lo, hi):
+        @pl.loop(lo, hi)
+        def _(k):
+            fd = (f + k) % 16
+            for t, (s, d) in enumerate(wpieces(f, fd, True)):
+                rc(s, d, sw.at[fd, t], rw.at[f, t], (r, fd)).start()
+
+    def ssend():
+        @pl.loop(1, 16)
+        def _(k):
+            fd = (f + k) % 16
+            rc(sm_ref, SM.at[f], ssm.at[fd], rsm.at[f], (r, fd)).start()
+
+    def wown():
+        for t, (s, d) in enumerate(wpieces(f, f, True)):
+            rc(s, d, sxw.at[f, t], rxw.at[f, t], xp).start()
+            lc(s, d, rw.at[f, t]).start()
+
     for cp in (own_x, own_b, load_o, load_s, own_s):
         cp.start()
-
-    @pl.loop(1, 16)
-    def _(k):
-        fd = (f + k) % 16
-        rc(sm_ref, SM.at[f], ssm.at[fd], rsm.at[f], (r, fd)).start()
-        for t, (s, d) in enumerate(wpieces(f, fd, True)):
-            rc(s, d, sw.at[fd, t], rw.at[f, t], (r, fd)).start()
-
-    for t, (s, d) in enumerate(wpieces(f, f, True)):
-        rc(s, d, sxw.at[f, t], rxw.at[f, t], xp).start()
-        lc(s, d, rw.at[f, t]).start()
-    xs(1)
-    xy(0)
-    fwd(1, 5)
-    xs(2)
-    xy(1)
-    fwd(5, 9)
-    xs(3)
-    xy(2)
-    fwd(9, 13)
-    gb()
-    xy(3)
+    ssend()
+    wsend(1, 16)
+    wown()
+    xo()
+    xz()
+    go()
+    fwd(1, 9)
     own_s.wait()
 
     @pl.loop(1, 16)
@@ -531,29 +531,9 @@
         pick = (place == lax.broadcasted_iota(jnp.int32, (128, 128), 1).astype(f32)).astype(f32)
         hi = lax.Precision.HIGHEST
         CT[rows] = jnp.dot(pick, ct_ref[...], precision=hi, preferred_element_type=f32)
-        ST[rows] = jnp.dot(pick, st_ref[...], precision=hi, preferred_element_type=f32)
-
-    fwd(13, 16)
-    own_x.wait()
-    xf()
-
-    @pl.loop(0, 16)
-    def _(i):
-        @pl.loop(0, 8, unroll=2)
-        def _(k):
-            w = ds(128 * i + 16 * k, 16)
-            v = X[w].astype(f32)
-            v = v - jnp.mean(v, -1, keepdims=True)
-            v = v * lax.rsqrt(jnp.mean(v * v, -1, keepdims=True) + epsilon)
-            X[w] = v.astype(bf)
-
-        @pl.when(i == 8)
-        def _():
-            gs(1)
-            gy(0)
-
-    gs(2)
-    gy(1)
+
+    fwd(9, 16)
+    xs(1)
 
     for t, (s, d) in enumerate(wpieces(f, f, True)):
         lc(s, d, rw.at[f, t]).wait()
@@ -572,7 +552,7 @@
 
     def columns(j):
         for v in range(4):
-            COL[v] = jnp.broadcast_to(SMF[pl.ds(16 * j + v, 1)], (128, 128)).T
+            PR[pl.ds(128 * v, 128)] = jnp.broadcast_to(SMF[pl.ds(16 * j + v, 1)], (128, 128)).T
 
     def fold(v):
         return v[:8] + v[8:]
@@ -587,7 +567,7 @@
         def _(k):
             w = ds(128 * j + 16 * k, 16)
             cw = ds(16 * k, 16)
-            g1, s1, g2, s2 = (COL[v, cw] for v in range(4))
+            g1, s1, g2, s2 = (PR[ds(128 * v + 16 * k, 16)] for v in range(4))
             for t in range(3):
                 l = pl.ds(128 * t, 128)
                 v = WJ[w, l].astype(f32)
@@ -608,12 +588,29 @@
 
     lane = lax.broadcasted_iota(jnp.int32, (16, 128), 1)
 
+    def angles(v, ln):
+        return jnp.where(ln < 32, v, 1.0), jnp.where(ln < 32, pltpu.roll(v, 96, 1), 0.0)
+
     def swap(v, ln):
         return jnp.where(ln < 16, pltpu.roll(v, 112, 1), pltpu.roll(v, 16, 1))
 
+    scale = HEAD_DIM ** (-0.5)
+    down = lax.broadcasted_iota(jnp.int32, (128, 128), 0)
+    across = lax.broadcasted_iota(jnp.int32, (128, 128), 1)
+
+    own_x.wait()
+
     @pl.loop(0, 4)
-    def _(i):
+    def _(p):
+        i = phys(jnp.where((zz == 1) & (p < 2), 1 - p, p))
         rows = ds(512 * i, 512)
+        pl.when((p > 0) & (p < 3))(lambda: xs(p + 1))
+        @pl.when(p == 1)
+        def _():
+            gz()
+
+        xy(p)
+        xl(i)
         T1[:, pl.ds(0, 384)] = mm(X[rows], WJ[...], 1, 0)
         T1[:, pl.ds(384, 512)] = mm(X[rows], WE[...], 1, 0)
 
@@ -621,7 +618,7 @@
         def _(k):
             w = ds(16 * k, 16)
             gw = ds(512 * i + 16 * k, 16)
-            cos, sin = CT[gw], ST[gw]
+            cos, sin = angles(CT[gw], lane)
             for t in range(2):
                 l = pl.ds(128 * t, 128)
                 v = T1[w, l] + CV[0:1, l]
@@ -637,32 +634,33 @@
                     part + v * jnp.exp(-0.5 * v * v) * 0.3989422804014327
                 ).astype(bf)
 
-        @pl.when(i == 1)
+        @pl.loop(0, 4, unroll=2)
+        def _(j):
+            slot = 4 * i + j
+            rows = ds(128 * slot, 128)
+            q = QKV[rows, pl.ds(0, 128)]
+            k = QKV[rows, pl.ds(128, 128)]
+            v = QKV[rows, pl.ds(256, 128)]
+            seg = jnp.broadcast_to(SMF[pl.ds(16 * slot + 9, 1)], (128, 128))
+            s = mm(q, k, 1, 1) * scale
+            s = jnp.where((seg == seg.T) & (across <= down), s, masked_score)
+            e = jnp.exp(s - jnp.max(s, -1, keepdims=True))
+            p = e / jnp.sum(e, -1, keepdims=True)
+            PR[rows] = p
+            INNER[rows, pl.ds(0, 128)] = mm(p.astype(bf), v, 1, 0).astype(bf)
+
+        @pl.when(p == 2)
         def _():
-            gs(3)
-            gy(2)
-
-        @pl.when(i == 3)
+            gs(1)
+            gy(0)
+
+        @pl.when(p == 3)
         def _():
-            gy(3)
-
-    scale = HEAD_DIM ** (-0.5)
-    down = lax.broadcasted_iota(jnp.int32, (128, 128), 0)
-    across = lax.broadcasted_iota(jnp.int32, (128, 128), 1)
-
-    @pl.loop(0, 16, unroll=2)
-    def _(i):
-        rows = ds(128 * i, 128)
-        q = QKV[rows, pl.ds(0, 128)]
-        k = QKV[rows, pl.ds(128, 128)]
-        v = QKV[rows, pl.ds(256, 128)]
-        seg = jnp.broadcast_to(SMF[pl.ds(16 * i + 9, 1)], (128, 128))
-        s = mm(q, k, 1, 1) * scale
-        s = jnp.where((seg == seg.T) & (across <= down), s, masked_score)
-        e = jnp.exp(s - jnp.max(s, -1, keepdims=True))
-        p = e / jnp.sum(e, -1, keepdims=True)
-        PR[rows] = p
-        INNER[rows, pl.ds(0, 128)] = mm(p.astype(bf), v, 1, 0).astype(bf)
+            gs(2)
+            gy(1)
+
+
+    xf()
 
     def add_into(dst, src, rows):
         @pl.loop(0, rows // 16)
@@ -681,8 +679,8 @@
             a_send(k).wait_recv()
             add_into(own(k), AA(k), 128)
 
-        def far():
-            for q in (3, 0, 2, 1):
+        def far(*turns):
+            for q in turns or (3, 0, 2, 1):
                 prep(phys(q) * 2 + 1 - y)
                 b_send(phys(q)).start()
 
@@ -708,13 +706,11 @@
 
         def step(q):
             near(q)
-            zp = phys(q)
-            k = zp * 2 + y
-
-            @pl.when(zz == 0)
-            def _():
-                if q > 0:
-                    send(q, f_in).start()
+            if q > 0:
+                pl.when(zz == 0)(lambda: send(q, f_in).start())
+
+        def relay(q):
+            k = phys(q) * 2 + y
 
             @pl.when(zz == 1)
             def _():
@@ -734,7 +730,8 @@
                 v = own(k)[w].astype(f32)
                 for b in bufs:
                     v = v + b[w].astype(f32)
-                STAGE[w] = v
+                for l, n in enumerate((896, 896, 256)):
+                    T1[ds(128 * l + 16 * i, 16), pl.ds(0, n)] = v[:, 896 * l : 896 * l + n]
 
         def last():
             @pl.when(zz == 0)
@@ -745,9 +742,14 @@
             def _():
                 total(1, [got(1), got(1, True)])
 
-            cp = lc(STAGE, SO, lsem.at[5])
-            cp.start()
-            cp.wait()
+            cps = [
+                lc(T1.at[pl.ds(128 * l, 128), pl.ds(0, n)], SO.at[:, pl.ds(896 * l, n)], lsem.at[at])
+                for l, n, at in ((0, 896, 5), (1, 896, 10), (2, 256, 11))
+            ]
+            for cp in cps:
+                cp.start()
+            for cp in cps:
+                cp.wait()
 
         def drain(first=0):
             @pl.loop(first, 8)
@@ -766,7 +768,7 @@
                 if q == 0:
                     pl.when(zz == 1)(lambda: send(q, f_out).wait_send())
 
-        return a_send, far, step, last, drain
+        return a_send, far, step, last, drain, relay
 
     R1 = reducer(
         0, lambda k: RING.at[k % 3], lambda k: L1.at[k], lambda k: A1.at[k], lambda k: B1.at[k],
@@ -776,10 +778,10 @@
         1,
         lambda k: BG.at[ds(128 * (2 * k + 1 - c), 128)],
         lambda k: BG.at[ds(128 * (2 * k + c), 128)],
-        lambda k: X.at[ds(128 * k, 128)],
-        lambda k: X.at[ds(1024 + 128 * k, 128)],
-        lambda k: X.at[ds(1536 + 128 * k, 128)],
-        C2X,
+        lambda k: A2.at[k],
+        lambda k: RING.at[k],
+        lambda k: WOS.at[ds(128 * k, 128)],
+        WOS.at[pl.ds(512, 128)],
         SO2,
     )
 
@@ -799,7 +801,15 @@
 
         R1[0](b).start()
 
+        @pl.when(b == 2)
+        def _():
+            gs(3)
+            gy(2)
+
+    gy(3)
     own_b.wait()
+    for q in range(4):
+        gl(q)
     gf()
 
     half = ds(320 * r, 320)
@@ -860,10 +870,19 @@
             SLOPE[gw] = e
             GBR[:, pl.ds(384, 512)] += fold(e.astype(f32))
 
+    @pl.loop(5, 8)
+    def _(b):
+        R1[0](b).wait_send()
+
+    for dev in (sib, yp, f_in):
+        pl.semaphore_signal(ready, inc=1, device_id=dev, device_id_type=MESH)
+
+    @pl.when(zz == 1)
+    def _():
+        pl.semaphore_signal(ready, inc=1, device_id=f_out, device_id_type=MESH)
+
     os_step(0)
-    R1[2](3)
     os_step(1)
-    R1[2](0)
 
     lane_b = lax.broadcasted_iota(jnp.int32, (128, 128), 1)
 
@@ -878,7 +897,7 @@
         vg = mm(p.astype(bf), mg, 0, 0)
         pg = mm(mg, v, 1, 1)
         sgr = (p * (pg - jnp.sum(pg * p, -1, keepdims=True))).astype(bf)
-        cos, sin = CT[rows], ST[rows]
+        cos, sin = angles(CT[rows], lane_b)
         qg = mm(sgr, k, 1, 0) * scale
         kg = mm(sgr, q, 0, 0) * scale
         for t, g in enumerate((qg, kg, vg)):
@@ -890,9 +909,7 @@
             GBR[:, l] += fold_rows(g.astype(f32), 128)
 
     os_step(2)
-    R1[2](2)
     os_step(3)
-    R1[2](1)
     GBR[...] = jnp.broadcast_to(jnp.sum(GBR[...], 0, keepdims=True), GBR.shape)
 
     keep = ds(64 * r, 64)
@@ -960,6 +977,15 @@
                 for t in range(4):
                     lc(piece_of(fs, t), place_of(f, t, keep), sg.at[fs, t]).wait()
 
+    @pl.when(zz == 1)
+    def _():
+        pl.semaphore_wait(ready, 4)
+
+    @pl.when(zz == 0)
+    def _():
+        pl.semaphore_wait(ready, 3)
+
+
     @pl.loop(0, 4)
     def _(i):
         left = X[:, ds(512 * i, 512)]
@@ -977,7 +1003,7 @@
                 gw = ds(128 * j + 16 * k, 16)
                 cw = ds(16 * k, 16)
                 for b, (first, count, W) in enumerate(((0, 3, WJ), (384, 4, WE))):
-                    g, sh = COL[2 * b, cw], COL[2 * b + 1, cw]
+                    g, sh = (PR[ds(256 * b + 128 * v + 16 * k, 16)] for v in range(2))
                     a1 = jnp.zeros((16, 128), f32)
                     a2 = jnp.zeros((16, 128), f32)
                     for t in range(count):
@@ -988,13 +1014,34 @@
                         wt = W[gw, pl.ds(128 * t, 128)].astype(f32)
                         a1 = a1 + wt * m
                         a2 = a2 + wt * bias
-                    VC[2 * b, cw] = jnp.sum(a1, -1, keepdims=True) / g
-                    VC[2 * b + 1, cw] = jnp.sum(a2, -1, keepdims=True) / g
+                    for v, a in ((2 * b, a1), (2 * b + 1, a2)):
+                        CT[ds(128 * v + 16 * k, 16)] = jnp.broadcast_to(jnp.sum(a, -1, keepdims=True) / g, (16, 128))
 
             for v in range(4):
-                VEC[j, pl.ds(v, 1)] = VC[v].T[0:1]
+                VEC[j, pl.ds(v, 1)] = CT[pl.ds(128 * v, 128)].T[0:1]
 
         x1(i).start()
+
+        turn_at = phys(jnp.where(i == 0, 3, jnp.where(i == 1, 0, 4 - i)))
+
+        @pl.loop(2 * turn_at, 2 * turn_at + 2)
+        def _(b):
+            part = ds(256 * b, 256)
+            BG[part] = (mm(QKV[part], WJ[...], 1, 1) + mm(SLOPE[part], WE[...], 1, 1)).astype(bf)
+            R2[0](b).start()
+
+        @pl.when(i == 0)
+        def _():
+            R1[2](3)
+
+        @pl.when(i == 1)
+        def _():
+            R1[2](0)
+
+        @pl.when(i == 2)
+        def _():
+            R1[2](2)
+            R1[5](3)
 
     def tile(fd, src):
         return rc(VEC.at[fd], VR.at[src], sv.at[fd], rv.at[src], (r, fd))
@@ -1010,25 +1057,12 @@
         tile((f + k) % 16, f).start()
 
     VR[f] = VEC[f]
-    R1[3]()
-
-    for dev in (sib, yp, f_in):
-        pl.semaphore_signal(ready, inc=1, device_id=dev, device_id_type=MESH)
-
-    @pl.when(zz == 1)
-    def _():
-        pl.semaphore_signal(ready, inc=1, device_id=f_out, device_id_type=MESH)
-        pl.semaphore_wait(ready, 4)
-
-    @pl.when(zz == 0)
-    def _():
-        pl.semaphore_wait(ready, 3)
-
-    @pl.loop(0, 8)
-    def _(b):
-        rows = ds(256 * b, 256)
-        BG[rows] = (mm(QKV[rows], WJ[...], 1, 1) + mm(SLOPE[rows], WE[...], 1, 1)).astype(bf)
-        R2[0](b).start()
+    je_group(0)
+    je_group(1)
+    R1[2](1)
+    R1[5](2)
+    R2[1](3)
+    R2[1](0)
 
     def total_rep():
         return rc(TOT, TX, st_, rt_, xp)
@@ -1039,21 +1073,25 @@
 
     TOT[pl.ds(0, 7)] = jnp.sum(VR[...], 0)[0:7]
     total_rep().start()
-    je_group(0)
-    je_group(1)
-    R2[1]()
+    R1[5](0)
     je_group(2)
+    R2[1](2)
+    R2[1](1)
     je_group(3)
+    R1[3]()
     R2[2](3)
+    R2[2](0)
     fwd_group(0)
-    R2[2](0)
+    R2[2](2)
+    R2[5](3)
     fwd_group(1)
-    R2[2](2)
+    R2[2](1)
+    R2[5](2)
     fwd_group(2)
-    R2[2](1)
+    R2[5](0)
     fwd_group(3)
     R2[3]()
-    R1[4](5)
+    R1[4](8)
     R2[4]()
     send_small.wait()
 
@@ -1074,7 +1112,7 @@
     je_drain()
 
 
-def layer_call(x, bg, sm, jw, ew, wo, ws, ct, st, eb):
+def layer_call(x, bg, sm, jw, ew, wo, ws, ct, eb):
     S = jax.ShapeDtypeStruct
     D = pltpu.SemaphoreType.DMA
     V = pltpu.VMEM
@@ -1086,16 +1124,16 @@
             S((128, WIDE), f32), S((128, WIDE), f32), S((640, WIDE), bf), S((128, 3 * WIDE), bf),
             S((128, 4 * WIDE), bf), S((16, 128), f32), S((256, 128), f32),
         ),
-        in_specs=[hbm] * 7 + [vm] * 3,
+        in_specs=[hbm] * 7 + [vm] * 2,
         out_specs=(hbm, hbm, hbm, hbm, hbm, vm, hbm),
         scratch_shapes=[
             V((TOK, WIDE), bf), V((TOK, WIDE), bf), V((WIDE, 384), bf), V((WIDE, 512), bf), V((640, WIDE), bf),
-            V((TOK, 640), bf), V((TOK, 384), bf), V((TOK, 512), bf), V((TOK, 128), f32), V((TOK, 128), f32),
-            V((TOK, 128), f32), V((8, 128, WIDE), bf), V((3, 128, WIDE), bf), V((8, 128, WIDE), bf),
-            V((4, 128, WIDE), bf), V((5, 128, WIDE), bf), V((128, WIDE), bf),
+            V((TOK, 640), bf), V((TOK, 384), bf), V((TOK, 512), bf), V((TOK, 128), f32),
+            V((TOK, 128), f32), V((8, 128, WIDE), bf), V((4, 128, WIDE), bf), V((8, 128, WIDE), bf),
+            V((4, 128, WIDE), bf), V((5, 128, WIDE), bf), V((8, 128, WIDE), bf),
             V((16, 128, 896), bf), V((16, 64, 896), bf), V((4, 640, 512), bf), V((4, 320, 512), bf),
-            V((128, WIDE), f32), V((512, 896), f32), V((16, 16, 128), bf), V((256, 128), f32),
-            V((8, 896), f32), V((8, 896), f32), V((4, 128, 128), f32), V((4, 128, 128), f32),
+            V((512, 896), f32), V((16, 16, 128), bf), V((256, 128), f32),
+            V((8, 896), f32), V((8, 896), f32),
             V((16, 8, 128), f32), V((16, 8, 128), f32), V((16, 128), f32), V((16, 128), f32), V((1, 128), f32),
         ]
         + [D((16,))] * 10 + [D((16, 4))] * 4 + [D((16,))] * 2
@@ -1104,7 +1142,7 @@
         compiler_params=pltpu.CompilerParams(
             collective_id=0, has_side_effects=True, vmem_limit_bytes=67043328
         ),
-    )(x, bg, sm, jw, ew, wo, ws, ct, st, eb)
+    )(x, bg, sm, jw, ew, wo, ws, ct, eb)
 
 
 def wide(a):
@@ -1116,10 +1154,8 @@
     power = np.arange(ROT // 2, dtype=np.float32) * np.float32(2.0) / np.float32(ROT)
     angle = place * np.power(np.float32(rotary_base), -power)
     cosine, sine = (np.cos(angle), np.sin(angle))
-    rest = HEAD_DIM - ROT
-    ct = np.concatenate([cosine, cosine, np.ones((length, rest))], 1)
-    st = np.concatenate([-sine, sine, np.zeros((length, rest))], 1)
-    return (jnp.asarray(ct, f32), jnp.asarray(st, f32))
+    rest = np.zeros((length, HEAD_DIM - 2 * ROT))
+    return jnp.asarray(np.concatenate([cosine, cosine, -sine, sine, rest], 1), f32)
 
 
 def head_body(
@@ -1167,18 +1203,18 @@
         for k in range(item.shape[0]):
             small = jnp.where(row == at, item[k : k + 1], small)
             at += 1
-    ct, st = turn_tables(own)
-    summed, hat_own, os_grad, joined_grad, expand_grad, sums, small_all = layer_call(
-        layer_input, branch_own, small, joined_weight, expand_weight, output_weight, shrink_weight,
-        ct, st, wide(expand_bias).reshape(1, -1),
-    )
-    small_all = small_all.reshape(n, 16, part)
-    bias = (small_all[:, 4] + small_all[:, 5]).reshape(width)
+    ct = turn_tables(own)
     rows_own = wide(layer_input)
-    layer_output = (rows_own + live_rows * (summed + bias)).astype(bf)
     centred = rows_own - jnp.mean(rows_own, -1, keepdims=True)
     inverse = lax.rsqrt(jnp.mean(centred * centred, -1, keepdims=True) + epsilon)
     normalized = centred * inverse
+    summed, hat_own, os_grad, joined_grad, expand_grad, sums, small_all = layer_call(
+        normalized.astype(bf), branch_own, small, joined_weight, expand_weight, output_weight, shrink_weight,
+        ct, wide(expand_bias).reshape(1, -1),
+    )
+    small_all = small_all.reshape(n, 16, part)
+    bias = (small_all[:, 4] + small_all[:, 5]).reshape(width)
+    layer_output = (rows_own + live_rows * (summed + bias)).astype(bf)
     row_grad = inverse * (
         hat_own
         - jnp.mean(hat_own, -1, keepdims=True)

time: 382 us -> 338 us (0.88); the launches traced: 375 us -> 336 us
  Pallas kernels: 346 us -> 308 us
    pallas_call x1, Pallas kernels: 346 us -> 308 us  [layer_call(): pl.pallas_call(layer_kernel, out_shape=(S((128, WIDE), f32), S((128, WIDE...]
where the time goes in v4:
time: 338 us; the launch traced here: 336 us
  Pallas kernels  308 us (91%)
  other arithmetic  19.7 us (6%)
  local copies, waits for them, and re-layouts  7.54 us (2%)
    pallas_call x1, Pallas kernels, layer_call(): pl.pallas_call(layer_kernel, out_shape=(S((128, WIDE), f32), S((128, WIDE...  308 us

profile of v4, /device:TPU:10, one launch (start us, length us, event | category | flops | bytes accessed | tf_op | source)
XLA Modules:
  0.0 336.4 jit_solution(8566705150894801101)
XLA Ops:
  0.6 0.0 copy-start.8
  0.7 0.8 fusion.13
  1.5 0.9 convert_reduce_fusion.1
  2.4 0.7 convert_bitcast_fusion
  3.1 1.4 select_select_fusion.sm_ref
  4.5 1.2 convert_reduce_fusion
  5.7 0.0 copy-start.4
  5.7 1.3 fusion.8
  7.1 0.0 copy-start.6
  7.1 0.7 convert_bitcast_fusion.1
  7.7 0.0 copy-done.4
  7.7 0.0 copy-start.7
  7.7 2.5 fusion.4
  10.3 0.0 copy-done.6
  10.3 0.0 copy-done.7
  10.3 0.0 copy-done.8
  10.3 0.6 reshape.111
  10.9 308.3 %shard_map.272 = (f32[128,2048]{1,0:T(8,128)}, f32[128,2048]{1,0:T(8,128)}, bf16[640,2048]{1,0:T(8,128)(2,1)}, bf16[128,6144]{1,0:T(8,128)(2,1)}, bf16[128,8192]...) custom-call(bf16[128,2048]{1,0:T(8,128)(2,1)} %get-tuple-element.50.x_ref, ...), custom_call_target="tpu_custom_call" | custom-call | tf_op jit(solution)/shard_map/pallas_call | solution.py:1121
  319.2 0.0 copy-start.1
  319.2 1.8 fusion.12
  321.0 0.9 slice_add_fusion
  321.9 0.0 copy-done.1
  322.0 0.0 copy-start.5
  322.0 0.0 copy-start
  322.0 3.2 fusion.10
  325.2 0.0 copy-done.5
  325.2 0.5 slice_bitcast_fusion.2
  325.7 0.0 copy-start.9
  325.7 0.6 slice_bitcast_fusion
  326.3 0.6 slice_bitcast_fusion.1
  326.9 0.0 copy-done
  326.9 2.5 slice.63
  329.4 0.0 copy-start.2
  329.4 1.1 slice.62
  330.5 0.9 copy-done.2
  331.4 0.0 copy-start.3
  331.4 2.4 convert_element_type.64
  333.9 0.0 copy-done.3
  333.9 2.0 convert_element_type.62
  335.8 0.0 copy-done.9
  335.8 0.5 copy.32
  (11 shorter events, 0.1 us)
Async XLA Ops:
  0.6 9.6 %copy-start.8 = (bf16[512]{0:T(512)(128)(2,1)S(1)}, bf16[512]{0:T(512)(128)(2,1)}, u32[]{:S(2)}) copy-start(bf16[512]{0:T(512)(128)(2,1)} %param.29) | copy-start | bytes 3076
  5.7 2.0 copy-start.4
  7.1 3.2 copy-start.6
  7.7 2.5 copy-start.7
  319.2 2.8 copy-start.1
  322.0 3.3 copy-start.5
  322.0 4.9 %copy-start = (bf16[640,2048]{1,0:T(8,128)(2,1)S(1)}, bf16[640,2048]{1,0:T(8,128)(2,1)}, u32[]{:S(2)}) copy-start(bf16[640,2048]{1,0:T(8,128)(2,1)} %get-tuple-element.26) | copy-start | bytes 7864324
  325.7 10.1 %copy-start.9 = (f32[128]{0:T(128)}, f32[128]{0:T(128)S(1)}, u32[]{:S(2)}) copy-start(f32[128]{0:T(128)S(1)} %get-tuple-element.79) | copy-start | bytes 1540
  329.4 2.0 copy-start.2
  331.4 2.4 copy-start.3

commit v5 on v4

--- a/solution.py
+++ b/solution.py
@@ -507,7 +507,7 @@
     xo()
     xz()
     go()
-    fwd(1, 9)
+    fwd(1, 13)
     own_s.wait()
 
     @pl.loop(1, 16)
@@ -532,7 +532,7 @@
         hi = lax.Precision.HIGHEST
         CT[rows] = jnp.dot(pick, ct_ref[...], precision=hi, preferred_element_type=f32)
 
-    fwd(9, 16)
+    fwd(13, 16)
     xs(1)
 
     for t, (s, d) in enumerate(wpieces(f, f, True)):
@@ -1058,11 +1058,11 @@
 
     VR[f] = VEC[f]
     je_group(0)
+    R2[1](3)
+    R2[1](0)
     je_group(1)
     R1[2](1)
     R1[5](2)
-    R2[1](3)
-    R2[1](0)
 
     def total_rep():
         return rc(TOT, TX, st_, rt_, xp)
@@ -1073,21 +1073,21 @@
 
     TOT[pl.ds(0, 7)] = jnp.sum(VR[...], 0)[0:7]
     total_rep().start()
+    R2[1](2)
+    R2[1](1)
     R1[5](0)
     je_group(2)
-    R2[1](2)
-    R2[1](1)
     je_group(3)
     R1[3]()
     R2[2](3)
+    fwd_group(0)
     R2[2](0)
-    fwd_group(0)
+    fwd_group(1)
     R2[2](2)
     R2[5](3)
-    fwd_group(1)
+    fwd_group(2)
     R2[2](1)
     R2[5](2)
-    fwd_group(2)
     R2[5](0)
     fwd_group(3)
     R2[3]()
@@ -1222,7 +1222,6 @@
     )
     input_grad = (seeds + row_grad).astype(bf)
 
-    os_grad = wide(os_grad)
     return (
         layer_output,
         input_grad,
@@ -1230,13 +1229,13 @@
         sums[1],
         wide(joined_grad),
         sums[4:7].reshape(-1),
-        os_grad[:part],
+        wide(os_grad[:part]),
         sums[7],
         sums[2],
         sums[3],
         wide(expand_grad),
         sums[8:12].reshape(-1),
-        os_grad[part:],
+        wide(os_grad[part:]),
         sums[7],
     )
 

time: 338 us -> 333 us (0.985)
  local copies, waits for them, and re-layouts: 7.54 us -> 3.03 us
  other arithmetic: 19.7 us -> 23.5 us
    convert_element_type x3 -> x5, other arithmetic: 5.08 us -> 8.69 us  [wide(): return a.astype(f32)]
    slice x2 -> x0, local copies, waits for them, and re-layouts: 3.61 us -> none  [the longest x1 2.54 us: head_body(): os_grad[part:]]
where the time goes in v5:
time: 333 us
  Pallas kernels  306 us (92%)
  other arithmetic  23.5 us (7%)
    pallas_call x1, Pallas kernels, layer_call(): pl.pallas_call(layer_kernel, out_shape=(S((128, WIDE), f32), S((128, WIDE...  306 us
    convert_element_type x5, other arithmetic, wide(): return a.astype(f32)  8.69 us

profile of v5, /device:TPU:10, one launch (start us, length us, event | category | flops | bytes accessed | tf_op | source)
XLA Modules:
  0.0 333.0 jit_solution(12732908717015133390)
XLA Ops:
  0.6 0.0 copy-start.7
  0.7 0.8 fusion.13
  1.5 0.9 convert_reduce_fusion.1
  2.4 0.7 convert_bitcast_fusion
  3.1 1.4 select_select_fusion.sm_ref
  4.5 1.2 convert_reduce_fusion
  5.7 0.0 copy-start.3
  5.7 1.3 fusion.8
  7.1 0.0 copy-start.5
  7.1 0.7 convert_bitcast_fusion.1
  7.7 0.0 copy-done.3
  7.7 0.0 copy-start.6
  7.7 2.5 fusion.4
  10.3 0.0 copy-done.5
  10.3 0.0 copy-done.6
  10.3 0.0 copy-done.7
  10.3 0.6 reshape.111
  10.9 305.7 %shard_map.272 = (f32[128,2048]{1,0:T(8,128)}, f32[128,2048]{1,0:T(8,128)}, bf16[640,2048]{1,0:T(8,128)(2,1)}, bf16[128,6144]{1,0:T(8,128)(2,1)}, bf16[128,8192]...) custom-call(bf16[128,2048]{1,0:T(8,128)(2,1)} %get-tuple-element.50.x_ref, ...), custom_call_target="tpu_custom_call" | custom-call | tf_op jit(solution)/shard_map/pallas_call | solution.py:1121
  316.6 0.0 copy-start.4
  316.6 0.0 copy-start
  316.6 1.9 fusion.12
  318.5 0.9 slice_add_fusion
  319.4 3.4 %fusion.10 = (bf16[128,2048]{1,0:T(8,128)(2,1)}, bf16[128,2048]{1,0:T(8,128)(2,1)}) fusion(bf16[128,2048]{1,0:T(8,128)(2,1)} %param.17, bf16[128,2048]{1,0:T(8,128)(2,1)} %param.32, f32[128,2048]{1,0:T(8,128)} %get-tuple-element.23, f32[128]{0:T(128)S(1)} %broadcast_multiply_fusion, f32[128]{0:T(128)S(1)} %broadcast_multiply_fusion.1, f32[128]{0:T(128)} %copy-done.5, ...), kind=kLoop, calls=%fused_computation.16 | loop fusion | flops 3670016 | bytes 4205056 | tf_op jit(solution)/shard_map/convert_element_type | solution.py:1223
  322.8 0.0 copy-done.4
  322.8 0.5 slice_bitcast_fusion.2
  323.3 0.0 copy-start.8
  323.3 0.6 slice_bitcast_fusion
  323.9 0.6 slice_bitcast_fusion.1
  324.5 0.0 copy-done
  324.5 0.0 copy-start.1
  324.5 2.5 slice_convert_fusion
  327.0 1.1 slice_convert_fusion.1
  328.1 0.0 copy-done.1
  328.1 0.0 copy-start.2
  328.1 2.4 convert_element_type.67
  330.5 0.0 copy-done.2
  330.5 2.0 convert_element_type.65
  332.5 0.0 copy-done.8
  332.5 0.5 copy.32
  (11 shorter events, 0.1 us)
Async XLA Ops:
  0.6 9.6 %copy-start.7 = (bf16[512]{0:T(512)(128)(2,1)S(1)}, bf16[512]{0:T(512)(128)(2,1)}, u32[]{:S(2)}) copy-start(bf16[512]{0:T(512)(128)(2,1)} %param.29) | copy-start | bytes 3076
  5.7 2.0 copy-start.3
  7.1 3.2 copy-start.5
  7.7 2.5 copy-start.6
  316.6 6.2 %copy-start.4 = (f32[16,128]{1,0:T(8,128)S(1)}, f32[16,128]{1,0:T(8,128)}, u32[]{:S(2)}) copy-start(f32[16,128]{1,0:T(8,128)} %get-tuple-element.24) | copy-start | bytes 24580
  316.6 7.9 %copy-start = (bf16[640,2048]{1,0:T(8,128)(2,1)S(1)}, bf16[640,2048]{1,0:T(8,128)(2,1)}, u32[]{:S(2)}) copy-start(bf16[640,2048]{1,0:T(8,128)(2,1)} %get-tuple-element.26) | copy-start | bytes 7864324
  323.3 9.2 %copy-start.8 = (f32[128]{0:T(128)}, f32[128]{0:T(128)S(1)}, u32[]{:S(2)}) copy-start(f32[128]{0:T(128)S(1)} %get-tuple-element.79) | copy-start | bytes 1540
  324.5 3.6 %copy-start.1 = (bf16[128,8192]{1,0:T(8,128)(2,1)S(1)}, bf16[128,8192]{1,0:T(8,128)(2,1)}, u32[]{:S(2)}) copy-start(bf16[128,8192]{1,0:T(8,128)(2,1)} %get-tuple-element.27) | copy-start | bytes 6291460
  328.1 2.4 copy-start.2

commit v6 on v5

--- a/solution.py
+++ b/solution.py
@@ -1042,6 +1042,7 @@
         def _():
             R1[2](2)
             R1[5](3)
+            R2[1](3)
 
     def tile(fd, src):
         return rc(VEC.at[fd], VR.at[src], sv.at[fd], rv.at[src], (r, fd))
@@ -1058,7 +1059,6 @@
 
     VR[f] = VEC[f]
     je_group(0)
-    R2[1](3)
     R2[1](0)
     je_group(1)
     R1[2](1)

time: 333 us -> 333 us (level)
  no operation moved by 1% of the time
where the time goes in v6:
time: 333 us
  Pallas kernels  306 us (92%)
  other arithmetic  23.5 us (7%)
    pallas_call x1, Pallas kernels, layer_call(): pl.pallas_call(layer_kernel, out_shape=(S((128, WIDE), f32), S((128, WIDE...  306 us
    convert_element_type x5, other arithmetic, wide(): return a.astype(f32)  8.69 us

profile of v6, /device:TPU:10, one launch (start us, length us, event | category | flops | bytes accessed | tf_op | source)
XLA Modules:
  0.0 332.9 jit_solution(3393722454669096903)
XLA Ops:
  0.6 0.0 copy-start.7
  0.7 0.8 fusion.13
  1.5 0.9 convert_reduce_fusion.1
  2.4 0.7 convert_bitcast_fusion
  3.1 1.4 select_select_fusion.sm_ref
  4.5 1.2 convert_reduce_fusion
  5.7 0.0 copy-start.3
  5.7 1.3 fusion.8
  7.1 0.0 copy-start.5
  7.1 0.7 convert_bitcast_fusion.1
  7.7 0.0 copy-done.3
  7.7 0.0 copy-start.6
  7.7 2.5 fusion.4
  10.3 0.0 copy-done.5
  10.3 0.0 copy-done.6
  10.3 0.0 copy-done.7
  10.3 0.6 reshape.111
  10.9 305.6 %shard_map.272 = (f32[128,2048]{1,0:T(8,128)}, f32[128,2048]{1,0:T(8,128)}, bf16[640,2048]{1,0:T(8,128)(2,1)}, bf16[128,6144]{1,0:T(8,128)(2,1)}, bf16[128,8192]...) custom-call(bf16[128,2048]{1,0:T(8,128)(2,1)} %get-tuple-element.50.x_ref, ...), custom_call_target="tpu_custom_call" | custom-call | tf_op jit(solution)/shard_map/pallas_call | solution.py:1121
  316.5 0.0 copy-start.4
  316.5 0.0 copy-start
  316.5 1.9 fusion.12
  318.4 0.9 slice_add_fusion
  319.3 3.4 %fusion.10 = (bf16[128,2048]{1,0:T(8,128)(2,1)}, bf16[128,2048]{1,0:T(8,128)(2,1)}) fusion(bf16[128,2048]{1,0:T(8,128)(2,1)} %param.17, bf16[128,2048]{1,0:T(8,128)(2,1)} %param.32, f32[128,2048]{1,0:T(8,128)} %get-tuple-element.23, f32[128]{0:T(128)S(1)} %broadcast_multiply_fusion, f32[128]{0:T(128)S(1)} %broadcast_multiply_fusion.1, f32[128]{0:T(128)} %copy-done.5, ...), kind=kLoop, calls=%fused_computation.16 | loop fusion | flops 3670016 | bytes 4205056 | tf_op jit(solution)/shard_map/convert_element_type | solution.py:1223
  322.7 0.0 copy-done.4
  322.7 0.5 slice_bitcast_fusion.2
  323.2 0.0 copy-start.8
  323.2 0.6 slice_bitcast_fusion
  323.8 0.6 slice_bitcast_fusion.1
  324.4 0.0 copy-done
  324.4 0.0 copy-start.1
  324.4 2.5 slice_convert_fusion
  326.9 1.1 slice_convert_fusion.1
  328.0 0.0 copy-done.1
  328.0 0.0 copy-start.2
  328.0 2.4 convert_element_type.67
  330.4 0.0 copy-done.2
  330.4 2.0 convert_element_type.65
  332.4 0.0 copy-done.8
  332.4 0.5 copy.32
  (11 shorter events, 0.1 us)
Async XLA Ops:
  0.6 9.6 %copy-start.7 = (bf16[512]{0:T(512)(128)(2,1)S(1)}, bf16[512]{0:T(512)(128)(2,1)}, u32[]{:S(2)}) copy-start(bf16[512]{0:T(512)(128)(2,1)} %param.29) | copy-start | bytes 3076
  5.7 2.0 copy-start.3
  7.1 3.2 copy-start.5
  7.7 2.5 copy-start.6
  316.5 6.2 %copy-start.4 = (f32[16,128]{1,0:T(8,128)S(1)}, f32[16,128]{1,0:T(8,128)}, u32[]{:S(2)}) copy-start(f32[16,128]{1,0:T(8,128)} %get-tuple-element.24) | copy-start | bytes 24580
  316.5 7.9 %copy-start = (bf16[640,2048]{1,0:T(8,128)(2,1)S(1)}, bf16[640,2048]{1,0:T(8,128)(2,1)}, u32[]{:S(2)}) copy-start(bf16[640,2048]{1,0:T(8,128)(2,1)} %get-tuple-element.26) | copy-start | bytes 7864324
  323.2 9.2 %copy-start.8 = (f32[128]{0:T(128)}, f32[128]{0:T(128)S(1)}, u32[]{:S(2)}) copy-start(f32[128]{0:T(128)S(1)} %get-tuple-element.79) | copy-start | bytes 1540
  324.4 3.6 %copy-start.1 = (bf16[128,8192]{1,0:T(8,128)(2,1)S(1)}, bf16[128,8192]{1,0:T(8,128)(2,1)}, u32[]{:S(2)}) copy-start(bf16[128,8192]{1,0:T(8,128)(2,1)} %get-tuple-element.27) | copy-start | bytes 6291460
  328.0 2.4 copy-start.2
